TPU v7x, 8 devices: a whole 2x2x1 slice. The times are simulated.
8 devices in a mesh: dp: 1 (over z), sp: 8 (over y, x, core).
Axes of the slice: x: 2, y: 2, z: 1, core: 2. Of those that a mesh axis runs over, the one named last changes fastest.
Arguments:
- patches: bfloat16 [2, 2048, 1536], P('dp', 'sp')
- vis_mask: int32 [2, 2048], P('dp', 'sp')
- enc_pos: bfloat16 [2048, 1280], P(('dp', 'sp'))
- dec_pos: bfloat16 [2048, 512], P(('dp', 'sp'))
- w_pe: bfloat16 [1536, 1280], replicated
- b_pe: bfloat16 [1280], replicated
- enc_qkv: bfloat16 [2, 1280, 3, 16, 80], replicated
- enc_proj: bfloat16 [2, 16, 80, 1280], replicated
- enc_up: bfloat16 [2, 1280, 5120], replicated
- enc_down: bfloat16 [2, 5120, 1280], replicated
- w_ed: bfloat16 [1280, 512], replicated
- mask_token: bfloat16 [512], replicated
- dec_qkv: bfloat16 [2, 512, 3, 16, 32], replicated
- dec_proj: bfloat16 [2, 16, 32, 512], replicated
- dec_up: bfloat16 [2, 512, 2048], replicated
- dec_down: bfloat16 [2, 2048, 512], replicated
- w_out: bfloat16 [512, 1536], replicated
Outputs:
- output: float32 [2, 2048, 1536], P('dp', 'sp')
All inputs are finite; a program needn't handle non-finite values.
Results may differ from a plain program's by a relative error of at most 0.0159664.
Values are sent between devices in bfloat16 or wider.
A program may use at most 1 GiB of HBM per device.

v0:
```python
import jax
import jax.numpy as jnp
from jax import lax
from jax.sharding import PartitionSpec as P

KEEP_DIV = 8


def layer_norm(hidden):
    hid_f32 = hidden.astype(jnp.float32)
    centred = hid_f32 - jnp.mean(hid_f32, axis=-1, keepdims=True)
    row_var = jnp.mean(centred * centred, axis=-1, keepdims=True)
    return (centred * lax.rsqrt(row_var + 1e-6)).astype(jnp.bfloat16)


def attn_mlp_block(hidden, w_qkv, w_proj, w_up, w_down):
    proj_qkv = jnp.einsum('cnd,dshk->scnhk', layer_norm(hidden), w_qkv, preferred_element_type=jnp.float32).astype(jnp.bfloat16)
    kv_all = lax.all_gather(proj_qkv[1:], 'sp', axis=2, tiled=True)
    scores = jnp.einsum('cqhk,cshk->chqs', proj_qkv[0], kv_all[0], preferred_element_type=jnp.float32) * proj_qkv.shape[-1] ** -0.5
    attn_probs = jax.nn.softmax(scores, axis=-1).astype(jnp.bfloat16)
    attended = jnp.einsum('chqs,cshk->cqhk', attn_probs, kv_all[1], preferred_element_type=jnp.float32).astype(jnp.bfloat16)
    mid_state = (hidden + jnp.einsum('cqhk,hkd->cqd', attended, w_proj, preferred_element_type=jnp.float32)).astype(jnp.bfloat16)
    up_act = jax.nn.gelu(jnp.einsum('cnd,df->cnf', layer_norm(mid_state), w_up, preferred_element_type=jnp.float32), approximate=False).astype(jnp.bfloat16)
    return (mid_state + jnp.einsum('cnf,fd->cnd', up_act, w_down, preferred_element_type=jnp.float32)).astype(jnp.bfloat16)


def solution(mesh):
    group_size = mesh.shape['sp']
    to_next = [(src_dev, src_dev + 1) for src_dev in range(group_size - 1)]
    to_prev = [(src_dev + 1, src_dev) for src_dev in range(group_size - 1)]

    def local_program(patches, vis_mask, enc_pos, dec_pos, w_pe, b_pe, enc_qkv, enc_proj, enc_up, enc_down, w_ed, mask_token, dec_qkv, dec_proj, dec_up, dec_down, w_out):
        vis_shard = patches.shape[1] // KEEP_DIV
        half_rows = vis_shard // 2
        my_index = lax.axis_index('sp')
        vis_counts = lax.all_gather(jnp.sum(vis_mask, axis=1), 'sp')
        vis_before = jnp.sum(jnp.where(jnp.arange(group_size)[:, None] < my_index, vis_counts, 0), axis=0)
        local_rank = jnp.cumsum(vis_mask, axis=1) - vis_mask
        dest_row = vis_before[:, None] + local_rank - my_index * vis_shard + half_rows
        row_ids = jnp.arange(2 * vis_shard)
        select = ((dest_row[:, None, :] == row_ids[None, :, None]) & (vis_mask[:, None, :] == 1)).astype(jnp.bfloat16)
        moved_x = jnp.einsum('cqi,cip->cqp', select, patches, preferred_element_type=jnp.float32).astype(jnp.bfloat16)
        moved_pos = jnp.einsum('cqi,id->cqd', select, enc_pos, preferred_element_type=jnp.float32)
        occupied = jnp.sum(select, axis=2, dtype=jnp.float32)
        embedded = (jnp.einsum('cqp,pd->cqd', moved_x, w_pe, preferred_element_type=jnp.float32)
                    + occupied[:, :, None] * b_pe.astype(jnp.float32) + moved_pos).astype(jnp.bfloat16)
        from_prev = lax.ppermute(embedded[:, 3 * half_rows:], 'sp', to_next)
        from_next = lax.ppermute(embedded[:, :half_rows], 'sp', to_prev)
        hidden = embedded[:, half_rows:3 * half_rows] + jnp.concatenate([from_prev, from_next], axis=1)
        for layer_idx in range(enc_qkv.shape[0]):
            hidden = attn_mlp_block(hidden, enc_qkv[layer_idx], enc_proj[layer_idx], enc_up[layer_idx], enc_down[layer_idx])
        z_enc = jnp.einsum('cnd,de->cne', layer_norm(hidden), w_ed, preferred_element_type=jnp.float32).astype(jnp.bfloat16)
        z_prev = lax.ppermute(z_enc[:, half_rows:], 'sp', to_next)
        z_next = lax.ppermute(z_enc[:, :half_rows], 'sp', to_prev)
        z_rows = jnp.concatenate([z_prev, z_enc, z_next], axis=1)
        placed = jnp.einsum('cqi,cqe->cie', select, z_rows, preferred_element_type=jnp.float32)
        masked_part = (1 - vis_mask).astype(jnp.float32)[:, :, None] * mask_token.astype(jnp.float32)
        hidden = (placed + masked_part + dec_pos.astype(jnp.float32)).astype(jnp.bfloat16)
        for layer_idx in range(dec_qkv.shape[0]):
            hidden = attn_mlp_block(hidden, dec_qkv[layer_idx], dec_proj[layer_idx], dec_up[layer_idx], dec_down[layer_idx])
        return jnp.einsum('cne,ep->cnp', layer_norm(hidden), w_out, preferred_element_type=jnp.float32)

    row_spec = P('dp', 'sp', None)
    pos_spec = P(('dp', 'sp'), None)
    arg_specs = (row_spec, P('dp', 'sp'), pos_spec, pos_spec) + (P(),) * 13
    return jax.shard_map(local_program, mesh=mesh, in_specs=arg_specs, out_specs=row_spec, check_vma=False)
```

profile of v0, /device:TPU:0, one launch (start us, length us, event | category | flops | bytes accessed | tf_op | source)
XLA Modules:
  0.0 435.7 jit_solution(6260883003811675475)
XLA Ops:
  9.1 25.0 %all-reduce = s32[16]{0:T(128)S(1)} all-reduce(s32[16]{0:T(128)S(1)} %dynamic-update-slice), channel_id=2, replica_groups=mesh['dp'=1,'sp'=8] {'sp'}, use_global_device_ids=true, to_apply=%add | all-reduce | flops 16 | bytes 128
  37.0 3.6 fusion.64
  43.5 4.4 %collective-permute-done.1 = bf16[2,16,1280]{2,1,0:T(8,128)(2,1)S(1)} collective-permute-done((bf16[2,16,1280]{2,1,0:T(8,128)(2,1)S(1)}, bf16[2,16,1280]{2,1,0:T(8,128)(2,1)S(1)}, u32[]{:S(2)}, u32[]{:S(2)}) %collective-permute-start.1) | collective-permute-done | bytes 81952 | tf_op jit(solution)/shard_map/ppermute | solution.py:48
  48.2 7.9 %fusion.184 = bf16[3,2,32,16,80]{4,2,3,0,1:T(8,128)(2,1)S(1)} fusion(bf16[2,1280,3,16,80]{1,4,3,2,0:T(8,128)(2,1)} %param.23, bf16[2,32,1280]{2,1,0:T(8,128)(2,1)S(1)} %get-tuple-element.14, f32[2,32]{1,0:T(2,128)S(1)} %add_rsqrt_fusion.9, f32[2,32]{1,0:T(2,128)S(1)} %broadcast_multiply_fusion.9), kind=kOutput, calls=%fused_computation.213 | convolution fusion | flops 629719040 | bytes 10486272 | tf_op jit(solution)/shard_map/cnd,dshk->scnhk/dot_general | solution.py:17
  57.3 35.0 %all-gather.6.cloned.1.call-done = bf16[2,2,256,16,80]{4,2,3,0,1:T(8,128)(2,1)} async-done(((bf16[2,2,32,16,80]{4,2,3,0,1:T(8,128)(2,1)}), bf16[2,2,256,16,80]{4,2,3,0,1:T(8,128)(2,1)}) %all-gather.6.cloned.1.call-update) | async-done | bytes 2621456 | tf_op jit(solution)/shard_map/all_gather | solution.py:18
  95.0 4.8 %fusion.511 = (f32[2,32]{1,0:T(2,128)S(1)}, f32[2,32,1280]{2,1,0:T(8,128)S(1)}) fusion(bf16[2,16,80,1280]{3,2,1,0:T(8,128)(2,1)} %param.24, bf16[2,2,256,16,80]{4,2,3,0,1:T(8,128)(2,1)} %all-gather.6.cloned.1.call-done, f32[2,16,32]{2,1,0:T(8,128)S(1)} %fusion.510, f32[2,16,32,256]{3,2,1,0:T(8,128)S(1)} %fusion.151, bf16[2,32,1280]{2,1,0:T(8,128)(2,1)} %copy-done.3), kind=kOutput, calls=%fused_computation.555 | convolution fusion | flops 252937408 | bytes 7979264 | tf_op jit(solution)/shard_map/cqhk,hkd->cqd/dot_general | solution.py:22
  100.1 6.5 %fusion.335 = (u8[32,5120]{1,0:T(8,128)(4,1)S(1)}, u8[32,5120]{1,0:T(8,128)(4,1)S(1)}, f32[2,32,5120]{2,1,0:T(8,128)S(1)}) fusion(bf16[2,1280,5120]{2,1,0:T(8,128)(2,1)} %param.25, f32[2,32,1280]{2,1,0:T(8,128)S(1)} %get-tuple-element.22, f32[2,32]{1,0:T(2,128)S(1)} %add_rsqrt_fusion.8, f32[2,32]{1,0:T(2,128)S(1)} %broadcast_multiply_fusion.8), kind=kOutput, calls=%fused_computation.357 | convolution fusion | flops 843038720 | bytes 15073792 | tf_op jit(solution)/shard_map/cnd,df->cnf/dot_general | solution.py:23
  106.6 7.8 %fusion.512 = (f32[2,32]{1,0:T(2,128)S(1)}, f32[2,32,1280]{2,1,0:T(8,128)S(1)}) fusion(f32[2,32,1280]{2,1,0:T(8,128)S(1)} %get-tuple-element.22, bf16[2,5120,1280]{2,1,0:T(8,128)(2,1)} %param.26, f32[2,32,5120]{2,1,0:T(8,128)S(1)} %get-tuple-element.23, u8[32,5120]{1,0:T(8,128)(4,1)S(1)} %get-tuple-element.12, u8[32,5120]{1,0:T(8,128)(4,1)S(1)} %get-tuple-element.11), kind=kOutput, calls=%fused_computation.556 | convolution fusion | flops 862126016 | bytes 15401216 | tf_op jit(solution)/shard_map/cnf,fd->cnd/dot_general | solution.py:24
  114.7 4.1 fusion.181
  120.0 31.4 %all-gather.8.cloned.1.call-done = bf16[2,2,256,16,80]{4,2,3,0,1:T(8,128)(2,1)} async-done(((bf16[2,2,32,16,80]{4,2,3,0,1:T(8,128)(2,1)}), bf16[2,2,256,16,80]{4,2,3,0,1:T(8,128)(2,1)}) %all-gather.8.cloned.1.call-update) | async-done | bytes 2621456 | tf_op jit(solution)/shard_map/all_gather | solution.py:18
  154.1 4.8 %fusion.514 = (f32[2,32]{1,0:T(2,128)S(1)}, f32[2,32,1280]{2,1,0:T(8,128)S(1)}) fusion(f32[2,32,1280]{2,1,0:T(8,128)} %copy-done.6, bf16[2,16,80,1280]{3,2,1,0:T(8,128)(2,1)} %param.24, bf16[2,2,256,16,80]{4,2,3,0,1:T(8,128)(2,1)} %all-gather.8.cloned.1.call-done, f32[2,16,32]{2,1,0:T(8,128)S(1)} %fusion.513, f32[2,16,32,256]{3,2,1,0:T(8,128)S(1)} %fusion.152), kind=kOutput, calls=%fused_computation.558 | convolution fusion | flops 252855488 | bytes 8143104 | tf_op jit(solution)/shard_map/cqhk,hkd->cqd/dot_general | solution.py:22
  159.1 6.4 %fusion.336 = (u8[32,5120]{1,0:T(8,128)(4,1)S(1)}, u8[32,5120]{1,0:T(8,128)(4,1)S(1)}, f32[2,32,5120]{2,1,0:T(8,128)S(1)}) fusion(bf16[2,1280,5120]{2,1,0:T(8,128)(2,1)} %param.25, f32[2,32,1280]{2,1,0:T(8,128)S(1)} %get-tuple-element.27, f32[2,32]{1,0:T(2,128)S(1)} %add_rsqrt_fusion.6, f32[2,32]{1,0:T(2,128)S(1)} %broadcast_multiply_fusion.6), kind=kOutput, calls=%fused_computation.358 | convolution fusion | flops 843038720 | bytes 15073792 | tf_op jit(solution)/shard_map/cnd,df->cnf/dot_general | solution.py:23
  165.5 7.7 %fusion.515 = (f32[2,32]{1,0:T(2,128)S(1)}, f32[2,32,1280]{2,1,0:T(8,128)S(1)}) fusion(f32[2,32,1280]{2,1,0:T(8,128)S(1)} %get-tuple-element.27, bf16[2,5120,1280]{2,1,0:T(8,128)(2,1)} %param.26, f32[2,32,5120]{2,1,0:T(8,128)S(1)} %get-tuple-element.28, u8[32,5120]{1,0:T(8,128)(4,1)S(1)} %get-tuple-element.10, u8[32,5120]{1,0:T(8,128)(4,1)S(1)} %get-tuple-element.9), kind=kOutput, calls=%fused_computation.559 | convolution fusion | flops 862126016 | bytes 15401216 | tf_op jit(solution)/shard_map/cnf,fd->cnd/dot_general | solution.py:24
  184.1 52.0 %all-gather.10.cloned.1.call-done = bf16[2,2,2048,16,32]{2,4,3,0,1:T(8,128)(2,1)} async-done(((bf16[2,2,256,16,32]{2,4,3,0,1:T(8,128)(2,1)}), bf16[2,2,2048,16,32]{2,4,3,0,1:T(8,128)(2,1)}) %all-gather.10.cloned.1.call-update) | async-done | bytes 8388624 | tf_op jit(solution)/shard_map/all_gather | solution.py:18
  236.2 28.3 %fusion.516 = (f32[2,16,256]{2,1,0:T(8,128)S(1)}, f32[2,16,256,2048]{3,2,1,0:T(8,128)}) fusion(bf16[2,2,2048,16,32]{2,4,3,0,1:T(8,128)(2,1)} %all-gather.10.cloned.1.call-done, bf16[3,2,256,16,32]{2,4,3,0,1:T(8,128)(2,1)S(1)} %fusion.136), kind=kOutput, calls=%fused_computation.560 | convolution fusion | flops 1124075520 | bytes 71860224 | tf_op jit(solution)/shard_map/sub | solution.py:20
  264.5 25.2 %convert_reduce_fusion.2 = (f32[2,256]{1,0:T(2,128)S(1)}, bf16[2,256,512]{2,1,0:T(8,128)(2,1)S(1)}) fusion(bf16[2,16,32,512]{3,2,1,0:T(8,128)(2,1)} %param.30, f32[2,16,256,2048]{3,2,1,0:T(8,128)} %get-tuple-element.34, f32[2,16,256]{2,1,0:T(8,128)S(1)} %get-tuple-element.33, bf16[2,2,2048,16,32]{2,4,3,0,1:T(8,128)(2,1)} %all-gather.10.cloned.1.call-done, ...), kind=kOutput, calls=%fused_computation.148 | convolution fusion | flops 1377304064 | bytes 72910848 | tf_op jit(solution)/shard_map/cqhk,hkd->cqd/dot_general | solution.py:22
  290.0 4.2 fusion.233
  294.3 10.0 %convert_reduce_fusion.1 = (f32[2,256]{1,0:T(2,128)S(1)}, bf16[2,256,512]{2,1,0:T(8,128)(2,1)S(1)}) fusion(bf16[2,2048,512]{2,1,0:T(8,128)(2,1)S(1)} %copy-done.9, f32[2,256,2048]{2,1,0:T(8,128)S(1)} %get-tuple-element.37, u8[256,2048]{1,0:T(8,128)(4,1)S(1)} %get-tuple-element.8, u8[256,2048]{1,0:T(8,128)(4,1)S(1)} %get-tuple-element.7, ...), kind=kOutput, calls=%fused_computation.145 | convolution fusion | flops 1148452352 | bytes 8390656 | tf_op jit(solution)/shard_map/cnf,fd->cnd/dot_general | solution.py:24
  307.4 50.1 %all-gather.12.cloned.1.call-done = bf16[2,2,2048,16,32]{2,4,3,0,1:T(8,128)(2,1)} async-done(((bf16[2,2,256,16,32]{2,4,3,0,1:T(8,128)(2,1)}), bf16[2,2,2048,16,32]{2,4,3,0,1:T(8,128)(2,1)}) %all-gather.12.cloned.1.call-update) | async-done | bytes 8388624 | tf_op jit(solution)/shard_map/all_gather | solution.py:18
  357.5 28.3 %fusion.517 = (f32[2,16,256]{2,1,0:T(8,128)S(1)}, f32[2,16,256,2048]{3,2,1,0:T(8,128)}) fusion(bf16[2,2,2048,16,32]{2,4,3,0,1:T(8,128)(2,1)} %all-gather.12.cloned.1.call-done, bf16[3,2,256,16,32]{2,4,3,0,1:T(8,128)(2,1)S(1)} %fusion.139), kind=kOutput, calls=%fused_computation.561 | convolution fusion | flops 1124075520 | bytes 71860224 | tf_op jit(solution)/shard_map/sub | solution.py:20
  385.8 25.5 %convert_reduce_fusion = (f32[2,256]{1,0:T(2,128)S(1)}, bf16[2,256,512]{2,1,0:T(8,128)(2,1)S(1)}) fusion(bf16[2,16,32,512]{3,2,1,0:T(8,128)(2,1)} %param.30, f32[2,16,256,2048]{3,2,1,0:T(8,128)} %get-tuple-element.41, f32[2,16,256]{2,1,0:T(8,128)S(1)} %get-tuple-element.40, bf16[2,2,2048,16,32]{2,4,3,0,1:T(8,128)(2,1)} %all-gather.12.cloned.1.call-done, ...), kind=kOutput, calls=%fused_computation.141 | convolution fusion | flops 1377304064 | bytes 72910848 | tf_op jit(solution)/shard_map/cqhk,hkd->cqd/dot_general | solution.py:22
  411.6 4.2 fusion.234
  415.8 9.8 %convert_reduce_fusion.4 = (f32[2,256]{1,0:T(2,128)S(1)}, bf16[2,256,512]{2,1,0:T(8,128)(2,1)S(1)}) fusion(bf16[2,2048,512]{2,1,0:T(8,128)(2,1)S(1)} %copy-done.10, f32[2,256,2048]{2,1,0:T(8,128)S(1)} %get-tuple-element.44, u8[256,2048]{1,0:T(8,128)(4,1)S(1)} %get-tuple-element.6, u8[256,2048]{1,0:T(8,128)(4,1)S(1)} %get-tuple-element.5, ...), kind=kOutput, calls=%fused_computation.168 | convolution fusion | flops 1148452352 | bytes 8390656 | tf_op jit(solution)/shard_map/cnf,fd->cnd/dot_general | solution.py:24
  426.0 2.7 fusion.128
  (115 shorter events, 31.8 us)
Async XLA Ops:
  6.5 419.4 %copy-start = (bf16[512,1536]{1,0:T(8,128)(2,1)S(1)}, bf16[512,1536]{1,0:T(8,128)(2,1)}, u32[]{:S(2)}) copy-start(bf16[512,1536]{1,0:T(8,128)(2,1)} %param.33) | copy-start | bytes 4718596
  6.5 34.1 %copy-start.2 = (bf16[256,1280]{1,0:T(8,128)(2,1)S(1)}, bf16[256,1280]{1,0:T(8,128)(2,1)}, u32[]{:S(2)}) copy-start(bf16[256,1280]{1,0:T(8,128)(2,1)} %param.19) | copy-start | bytes 1966084
  6.5 85.8 %all-gather.6.cloned.1.call-start = ((), (), s32[]{:S(2)}) async-start(), calls=%async_computation | async-start | bytes 4718592 | tf_op jit(solution)/shard_map/all_gather | solution.py:18
  40.9 2.6 collective-permute-start
  42.2 5.7 %collective-permute-start.1 = (bf16[2,16,1280]{2,1,0:T(8,128)(2,1)S(1)}, bf16[2,16,1280]{2,1,0:T(8,128)(2,1)S(1)}, u32[]{:S(2)}, u32[]{:S(2)}) collective-permute-start(bf16[2,16,1280]{2,1,0:T(8,128)(2,1)S(1)} %get-tuple-element.16), channel_id=1, source_target_pairs={{1,0},{2,1},{3,2},{4,3},{5,4},{6,5},{7,6}} | collective-permute-start | bytes 245768 | tf_op jit(solution)/shard_map/ppermute | solution.py:48
  48.0 8.1 %copy-start.3 = (bf16[2,32,1280]{2,1,0:T(8,128)(2,1)}, bf16[2,32,1280]{2,1,0:T(8,128)(2,1)S(1)}, u32[]{:S(2)}) copy-start(bf16[2,32,1280]{2,1,0:T(8,128)(2,1)S(1)} %get-tuple-element.14) | copy-start | bytes 491524
  57.0 94.3 %all-gather.8.cloned.1.call-start = ((), (), s32[]{:S(2)}) async-start(), calls=%async_computation.1 | async-start | bytes 4718592 | tf_op jit(solution)/shard_map/all_gather | solution.py:18
  100.0 14.6 %slice-start = ((s8[19660800]{0:T(1024)(128)(4,1)}), s8[4194304]{0:T(1024)(128)(4,1)S(1)}, s32[]{:S(2)}) async-start(s8[19660800]{0:T(1024)(128)(4,1)} %bitcast.357), calls=%async_computation.4 | async-start | bytes 8388608
  100.1 14.5 %slice-start.1 = ((s8[19660800]{0:T(1024)(128)(4,1)}), s8[4194304]{0:T(1024)(128)(4,1)S(1)}, s32[]{:S(2)}) async-start(s8[19660800]{0:T(1024)(128)(4,1)} %bitcast.357), calls=%async_computation.5 | async-start | bytes 8388608
  106.6 8.0 %slice-start.2 = ((s8[19660800]{0:T(1024)(128)(4,1)}), s8[4194304]{0:T(1024)(128)(4,1)S(1)}, s32[]{:S(2)}) async-start(s8[19660800]{0:T(1024)(128)(4,1)} %bitcast.357), calls=%async_computation.6 | async-start | bytes 8388608
  106.6 8.0 %slice-start.3 = ((s8[19660800]{0:T(1024)(128)(4,1)}), s8[4194304]{0:T(1024)(128)(4,1)S(1)}, s32[]{:S(2)}) async-start(s8[19660800]{0:T(1024)(128)(4,1)} %bitcast.357), calls=%async_computation.7 | async-start | bytes 8388608
  106.6 8.1 %slice-start.4 = ((s8[19660800]{0:T(1024)(128)(4,1)}), s8[2883584]{0:T(1024)(128)(4,1)S(1)}, s32[]{:S(2)}) async-start(s8[19660800]{0:T(1024)(128)(4,1)} %bitcast.357), calls=%async_computation.8 | async-start | bytes 5767168
  114.4 4.4 %copy-start.6 = (f32[2,32,1280]{2,1,0:T(8,128)}, f32[2,32,1280]{2,1,0:T(8,128)S(1)}, u32[]{:S(2)}) copy-start(f32[2,32,1280]{2,1,0:T(8,128)S(1)} %get-tuple-element.25) | copy-start | bytes 983044
  119.7 116.5 %all-gather.10.cloned.1.call-start = ((), (), s32[]{:S(2)}) async-start(), calls=%async_computation.2 | async-start | bytes 9437184 | tf_op jit(solution)/shard_map/all_gather | solution.py:18
  165.5 8.0 %copy-start.1 = (bf16[1280,512]{1,0:T(8,128)(2,1)S(1)}, bf16[1280,512]{1,0:T(8,128)(2,1)}, u32[]{:S(2)}) copy-start(bf16[1280,512]{1,0:T(8,128)(2,1)} %param.27) | copy-start | bytes 3932164
  165.5 12.0 %copy-start.8 = (bf16[512]{0:T(512)(128)(2,1)S(1)}, bf16[512]{0:T(512)(128)(2,1)}, u32[]{:S(2)}) copy-start(bf16[512]{0:T(512)(128)(2,1)} %param.28) | copy-start | bytes 3076
  165.5 12.0 %copy-start.7 = (bf16[256,512]{1,0:T(8,128)(2,1)S(1)}, bf16[256,512]{1,0:T(8,128)(2,1)}, u32[]{:S(2)}) copy-start(bf16[256,512]{1,0:T(8,128)(2,1)} %param.20) | copy-start | bytes 786436
  173.2 8.1 %copy-start.11 = (bf16[2,512,3,16,32]{1,4,3,2,0:T(8,128)(2,1)S(1)}, bf16[2,512,3,16,32]{1,4,3,2,0:T(8,128)(2,1)}, u32[]{:S(2)}) copy-start(bf16[2,512,3,16,32]{1,4,3,2,0:T(8,128)(2,1)} %param.29) | copy-start | bytes 9437188
  173.9 3.7 collective-permute-start.2
  176.2 3.9 collective-permute-start.3
  183.6 173.9 %all-gather.12.cloned.1.call-start = ((), (), s32[]{:S(2)}) async-start(), calls=%async_computation.3 | async-start | bytes 9437184 | tf_op jit(solution)/shard_map/all_gather | solution.py:18
  290.0 4.2 copy-start.9
  294.3 10.9 %copy-start.12 = (bf16[2,512,3,16,32]{1,4,3,2,0:T(8,128)(2,1)S(1)}, bf16[2,512,3,16,32]{1,4,3,2,0:T(8,128)(2,1)}, u32[]{:S(2)}) copy-start(bf16[2,512,3,16,32]{1,4,3,2,0:T(8,128)(2,1)} %param.29) | copy-start | bytes 9437188
  411.6 4.2 copy-start.10
  (2 other events, 1.7 us)
Sparse Core Ops, SparseCore 0:
  57.1 35.1 all-gather.5
  119.8 31.5 all-gather.7
  183.7 52.3 all-gather.9
  307.5 49.9 all-gather.11
where the time goes:
time: 440 us; the launch traced here: 436 us
  matrix products  200 us (45%)
  waiting for transfers between devices  176 us (40%)
  blocking collectives  25 us (6%)
  between operations  14.1 us (3%)
  other arithmetic  7.62 us (2%)
  starting transfers between devices  7.23 us (2%)
  local copies, waits for them, and re-layouts  6.13 us (1%)
    all_gather x4, waiting for transfers between devices, attn_mlp_block(): kv_all = lax.all_gather(proj_qkv[1:], 'sp', axis=2, tiled=True)  169 us
    dot_general x4, matrix products, attn_mlp_block(): jnp.einsum('cqhk,hkd->cqd', attended, w_proj, preferred_element_type=jnp....  60.3 us
    sub x2, matrix products, attn_mlp_block(): attn_probs = jax.nn.softmax(scores, axis=-1).astype(jnp.bfloat16)  56.6 us
    dot_general x4, matrix products, attn_mlp_block(): jnp.einsum('cnf,fd->cnd', up_act, w_down, preferred_element_type=jnp.floa...  35.3 us
    unnamed x1, blocking collectives  25 us
    dot_general x4, matrix products, attn_mlp_block(): jnp.einsum('cnd,df->cnf', layer_norm(mid_state), w_up, preferred_element_...  21.3 us
    dot_general x4, matrix products, attn_mlp_block(): jnp.einsum('cnd,dshk->scnhk', layer_norm(hidden), w_qkv, preferred_elemen...  14.3 us
  transfers between devices with their start and end apart: 8, of which 6 were waited for; matrix products, arithmetic and copies ran while one was open for 0% of the time, Pallas kernels for 0%

commit v1 on v0

--- a/solution.py
+++ b/solution.py
@@ -1,9 +1,193 @@
+import functools
+
 import jax
 import jax.numpy as jnp
 from jax import lax
+from jax.experimental import pallas as pl
+from jax.experimental.pallas import tpu as pltpu
 from jax.sharding import PartitionSpec as P
 
 KEEP_DIV = 8
+
+BF = jnp.bfloat16
+F32 = jnp.float32
+NT = (((1,), (1,)), ((), ()))
+TN = (((0,), (0,)), ((), ()))
+NN = (((1,), (0,)), ((), ()))
+LOG2E = 1.4426950408889634
+MESH = pl.DeviceIdType.MESH
+VMEM = pl.BlockSpec(memory_space=pltpu.VMEM)
+ANY = pl.BlockSpec(memory_space=pl.ANY)
+
+
+def mm(lhs, rhs, dims=NN):
+    return lax.dot_general(lhs, rhs, dims, preferred_element_type=F32)
+
+
+def norm_rows(hidden):
+    wide = hidden.astype(F32)
+    centred = wide - jnp.mean(wide, axis=-1, keepdims=True)
+    var = jnp.mean(centred * centred, axis=-1, keepdims=True)
+    return (centred * lax.rsqrt(var + 1e-6)).astype(BF)
+
+
+def gelu(x):
+    return 0.5 * x * (1.0 + lax.erf(x * 0.7071067811865476))
+
+
+def attend_clip(tok, rows, heads, hd, k_s, vt_s, q_s, s_s, o_s):
+    c2 = hd ** -0.5 * LOG2E
+    group = 256 // hd
+    chunk = 256
+    n_chunks = tok // chunk
+
+    def q_of(h):
+        g = h // group
+        qg = q_s[pl.ds(pl.multiple_of(g * 256, 256), 256), :]
+        row_head = lax.broadcasted_iota(jnp.int32, (256, rows), 0) // hd
+        return jnp.where(row_head == h - g * group, qg, jnp.zeros_like(qg)), pl.multiple_of(g * 256, 256)
+
+    def scores(h, slot):
+        qz, g0 = q_of(h)
+        top = None
+        for j in range(n_chunks):
+            s = mm(k_s[j * chunk:(j + 1) * chunk, pl.ds(g0, 256)], qz)
+            s_s[slot, j * chunk:(j + 1) * chunk, :] = s
+            t = jnp.max(s.reshape(chunk // 8, 8, rows), axis=0)
+            top = t if top is None else jnp.maximum(top, t)
+        return top
+
+    def finish(h, slot, top):
+        m = jnp.max(top, axis=0, keepdims=True) * c2
+        total = None
+        acc = None
+        v0 = pl.multiple_of(h * hd, hd)
+        for j in range(n_chunks):
+            e = jnp.exp2(s_s[slot, j * chunk:(j + 1) * chunk, :] * c2 - m)
+            t = jnp.sum(e.reshape(chunk // 8, 8, rows), axis=0)
+            total = t if total is None else total + t
+            a = mm(vt_s[pl.ds(v0, hd), j * chunk:(j + 1) * chunk], e.astype(BF))
+            acc = a if acc is None else acc + a
+        denom = jnp.sum(total, axis=0, keepdims=True)
+        o_s[pl.ds(v0, hd), :] = (acc / denom).astype(BF)
+
+    first = scores(0, 0)
+
+    def body(i, top0):
+        h = 2 * i
+        top1 = scores(h + 1, 1)
+        finish(h, 0, top0)
+        nxt = scores(jnp.minimum(h + 2, heads - 1), 0)
+        finish(h + 1, 1, top1)
+        return nxt
+
+    lax.fori_loop(0, heads // 2, body, first)
+
+
+def dec_kernel(last, n_clips, sp, a_all, u_in, wqkv, wproj, wup, wdown, wout, *rest):
+    if last:
+        out, k_s, vt_s, q_s, s_s, o_s = rest
+    else:
+        out, a_out, k_s, vt_s, q_s, s_s, o_s = rest
+    rows = u_in.shape[1]
+    width = u_in.shape[2]
+    tok = rows * sp
+    heads, hd = 16, width // 16
+    me = lax.axis_index('sp')
+
+    def clip(c, carry):
+        def kv(b, cc):
+            at = pl.multiple_of(b * rows, rows)
+            blk = a_all[b, c]
+            k_s[pl.ds(at, rows), :] = mm(blk, wqkv[width:2 * width, :], NT).astype(BF)
+            vt_s[:, pl.ds(at, rows)] = mm(wqkv[2 * width:, :], blk, NT).astype(BF)
+            return cc
+
+        lax.fori_loop(0, sp, kv, 0)
+        q_s[...] = mm(wqkv[:width, :], a_all[me, c], NT).astype(BF)
+        attend_clip(tok, rows, heads, hd, k_s, vt_s, q_s, s_s, o_s)
+        h1 = (u_in[c].astype(F32) + mm(o_s[...], wproj[...], TN)).astype(BF)
+        g = gelu(mm(norm_rows(h1), wup[...])).astype(BF)
+        u2 = (h1.astype(F32) + mm(g, wdown[...])).astype(BF)
+        a2 = norm_rows(u2)
+        if last:
+            out[c] = mm(a2, wout[...])
+        else:
+            out[c] = u2
+            a_out[c] = a2
+        return carry
+
+    lax.fori_loop(0, n_clips, clip, 0)
+
+
+def dec_layer(last, sp, a_all, u_in, wqkv, wproj, wup, wdown, wout):
+    n_clips, rows, width = u_in.shape
+    tok = rows * sp
+    if last:
+        shape = jax.ShapeDtypeStruct((n_clips, rows, wout.shape[1]), F32)
+        specs = VMEM
+    else:
+        shape = (jax.ShapeDtypeStruct(u_in.shape, BF),) * 2
+        specs = (VMEM, VMEM)
+    return pl.pallas_call(
+        functools.partial(dec_kernel, last, n_clips, sp),
+        out_shape=shape,
+        in_specs=[VMEM] * 7,
+        out_specs=specs,
+        scratch_shapes=[
+            pltpu.VMEM((tok, width), BF),
+            pltpu.VMEM((width, tok), BF),
+            pltpu.VMEM((width, rows), BF),
+            pltpu.VMEM((2, tok, rows), F32),
+            pltpu.VMEM((width, rows), BF),
+        ],
+        compiler_params=pltpu.CompilerParams(vmem_limit_bytes=60 << 20),
+        name='dec_last' if last else 'dec_first',
+    )(a_all, u_in, wqkv, wproj, wup, wdown, wout)
+
+
+def gather_kernel(sp, x_ref, all_ref, send_a, recv_a, send_b, recv_b, loc):
+    me = lax.axis_index('sp')
+    partner = me + 1 - 2 * lax.rem(me, 2)
+    barrier = pltpu.get_barrier_semaphore()
+    for k in range(1, sp):
+        pl.semaphore_signal(barrier, inc=1, device_id={'sp': lax.rem(me + k, sp)}, device_id_type=MESH)
+    pl.semaphore_wait(barrier, sp - 1)
+    own = pltpu.make_async_copy(x_ref, all_ref.at[me], loc)
+    own.start()
+    far = []
+    near = []
+    for k in range(sp // 2):
+        near.append(pltpu.make_async_remote_copy(
+            src_ref=x_ref if k == 0 else all_ref.at[lax.rem(me + sp - 2 * k, sp)],
+            dst_ref=all_ref.at[lax.rem(me + sp - 2 * k, sp)],
+            send_sem=send_b.at[k], recv_sem=recv_b.at[k], device_id={'sp': partner}, device_id_type=MESH))
+        if k:
+            far.append(pltpu.make_async_remote_copy(
+                src_ref=x_ref, dst_ref=all_ref.at[me], send_sem=send_a.at[k], recv_sem=recv_a.at[k],
+                device_id={'sp': lax.rem(me + 2 * k, sp)}, device_id_type=MESH))
+            far[-1].start()
+    near[0].start()
+    for k in range(1, sp // 2):
+        far[k - 1].wait_recv()
+        near[k].start()
+    for k in range(sp // 2):
+        near[k].wait()
+    for f in far:
+        f.wait_send()
+    own.wait()
+
+
+def gather(sp, x):
+    return pl.pallas_call(
+        functools.partial(gather_kernel, sp),
+        out_shape=jax.ShapeDtypeStruct((sp,) + x.shape, x.dtype),
+        in_specs=[VMEM],
+        out_specs=VMEM,
+        scratch_shapes=[pltpu.SemaphoreType.DMA((sp // 2,))] * 4 + [pltpu.SemaphoreType.DMA],
+        compiler_params=pltpu.CompilerParams(collective_id=0, has_side_effects=True),
+        name='gather_rows',
+    )(x)
 
 
 def layer_norm(hidden):
@@ -56,9 +240,17 @@
         placed = jnp.einsum('cqi,cqe->cie', select, z_rows, preferred_element_type=jnp.float32)
         masked_part = (1 - vis_mask).astype(jnp.float32)[:, :, None] * mask_token.astype(jnp.float32)
         hidden = (placed + masked_part + dec_pos.astype(jnp.float32)).astype(jnp.bfloat16)
-        for layer_idx in range(dec_qkv.shape[0]):
-            hidden = attn_mlp_block(hidden, dec_qkv[layer_idx], dec_proj[layer_idx], dec_up[layer_idx], dec_down[layer_idx])
-        return jnp.einsum('cne,ep->cnp', layer_norm(hidden), w_out, preferred_element_type=jnp.float32)
+        n_layers, d_width = dec_qkv.shape[:2]
+        wqkv_t = jnp.transpose(dec_qkv, (0, 2, 3, 4, 1)).reshape(n_layers, 3 * d_width, d_width)
+        wproj = dec_proj.reshape(n_layers, d_width, d_width)
+        acts = layer_norm(hidden)
+        for layer_idx in range(n_layers):
+            last = layer_idx == n_layers - 1
+            a_all = gather(group_size, acts)
+            res = dec_layer(last, group_size, a_all, hidden, wqkv_t[layer_idx], wproj[layer_idx], dec_up[layer_idx], dec_down[layer_idx], w_out)
+            if not last:
+                hidden, acts = res
+        return res
 
     row_spec = P('dp', 'sp', None)
     pos_spec = P(('dp', 'sp'), None)

time: 440 us -> 336 us (0.76)
  Pallas kernels: 0 us -> 146 us
  matrix products: 200 us -> 59.5 us
  waiting for transfers between devices: 176 us -> 62.5 us
  local copies, waits for them, and re-layouts: 6.13 us -> 14.3 us
    pallas_call x0 -> x4, Pallas kernels: none -> 146 us  [the longest x2 81 us: dec_layer(): pl.pallas_call(functools.partial(dec_kernel, last, n_clips, sp), out_shap...]
    all_gather x4 -> x2, waiting for transfers between devices: 169 us -> 56.7 us  [attn_mlp_block(): kv_all = lax.all_gather(proj_qkv[1:], 'sp', axis=2, tiled=True)]
    sub x2 -> x0, matrix products: 56.6 us -> none  [attn_mlp_block(): attn_probs = jax.nn.softmax(scores, axis=-1).astype(jnp.bfloat16)]
    dot_general x4 -> x2, matrix products: 60.3 us -> 9.57 us  [attn_mlp_block(): jnp.einsum('cqhk,hkd->cqd', attended, w_proj, preferred_element_type=jnp....]
    dot_general x4 -> x2, matrix products: 35.3 us -> 15.7 us  [attn_mlp_block(): jnp.einsum('cnf,fd->cnd', up_act, w_down, preferred_element_type=jnp.floa...]
    dot_general x4 -> x2, matrix products: 21.3 us -> 13.1 us  [attn_mlp_block(): jnp.einsum('cnd,df->cnf', layer_norm(mid_state), w_up, preferred_element_...]
    slice x1 -> x3, local copies, waits for them, and re-layouts: 0.21 us -> 5.5 us  [the longest x1 4.2 us: local_program(): wqkv_t[layer_idx]]
    squeeze x0 -> x2, local copies, waits for them, and re-layouts: none -> 4.97 us  [the longest x1 2.66 us: local_program(): dec_up[layer_idx]]
  transfers between devices with their start and end apart: 8 -> 6, of which waited for: 6 -> 4; matrix products, arithmetic and copies ran while one was open for 0% -> 3% of each run, Pallas kernels for 0% -> 0%
where the time goes in v1:
time: 336 us; the launch traced here: 335 us
  Pallas kernels  146 us (43%)
  waiting for transfers between devices  62.5 us (19%)
  matrix products  59.5 us (18%)
  blocking collectives  25 us (7%)
  local copies, waits for them, and re-layouts  14.3 us (4%)
  between operations  13.8 us (4%)
  other arithmetic  7.33 us (2%)
  starting transfers between devices  6.21 us (2%)
    pallas_call x2, Pallas kernels, dec_layer(): pl.pallas_call(functools.partial(dec_kernel, last, n_clips, sp), out_shap...  81 us
    pallas_call x2, Pallas kernels, gather(): pl.pallas_call(functools.partial(gather_kernel, sp), out_shape=jax.ShapeD...  65.3 us
    all_gather x2, waiting for transfers between devices, attn_mlp_block(): kv_all = lax.all_gather(proj_qkv[1:], 'sp', axis=2, tiled=True)  56.7 us
    unnamed x1, blocking collectives  25 us
    dot_general x2, matrix products, attn_mlp_block(): jnp.einsum('cnf,fd->cnd', up_act, w_down, preferred_element_type=jnp.floa...  15.7 us
    dot_general x2, matrix products, attn_mlp_block(): jnp.einsum('cnd,df->cnf', layer_norm(mid_state), w_up, preferred_element_...  13.1 us
    dot_general x2, matrix products, attn_mlp_block(): jnp.einsum('cnd,dshk->scnhk', layer_norm(hidden), w_qkv, preferred_elemen...  12 us
    dot_general x2, matrix products, attn_mlp_block(): jnp.einsum('cqhk,hkd->cqd', attended, w_proj, preferred_element_type=jnp....  9.57 us
  transfers between devices with their start and end apart: 6, of which 4 were waited for; matrix products, arithmetic and copies ran while one was open for 3% of the time, Pallas kernels for 0%

profile of v1, /device:TPU:0, one launch (start us, length us, event | category | flops | bytes accessed | tf_op | source)
XLA Modules:
  0.0 335.0 jit_solution(5558736928064353540)
XLA Ops:
  9.1 25.0 %all-reduce = s32[16]{0:T(128)S(1)} all-reduce(s32[16]{0:T(128)S(1)} %dynamic-update-slice), channel_id=2, replica_groups=mesh['dp'=1,'sp'=8] {'sp'}, use_global_device_ids=true, to_apply=%add | all-reduce | flops 16 | bytes 128
  37.0 3.2 fusion.28
  43.1 4.4 %collective-permute-done.1 = bf16[2,16,1280]{2,1,0:T(8,128)(2,1)S(1)} collective-permute-done((bf16[2,16,1280]{2,1,0:T(8,128)(2,1)S(1)}, bf16[2,16,1280]{2,1,0:T(8,128)(2,1)S(1)}, u32[]{:S(2)}, u32[]{:S(2)}) %collective-permute-start.1) | collective-permute-done | bytes 81952 | tf_op jit(solution)/shard_map/ppermute | solution.py:232
  47.8 7.9 %fusion.114 = bf16[3,2,32,16,80]{4,2,3,0,1:T(8,128)(2,1)S(1)} fusion(bf16[2,1280,3,16,80]{1,4,3,2,0:T(8,128)(2,1)} %param.23, bf16[2,32,1280]{2,1,0:T(8,128)(2,1)S(1)} %get-tuple-element.14, f32[2,32]{1,0:T(2,128)S(1)} %add_rsqrt_fusion.5, f32[2,32]{1,0:T(2,128)S(1)} %broadcast_multiply_fusion.5), kind=kOutput, calls=%fused_computation.116 | convolution fusion | flops 629719040 | bytes 10486272 | tf_op jit(solution)/shard_map/cnd,dshk->scnhk/dot_general | solution.py:201
  56.6 35.2 %all-gather.4.cloned.1.call-done = bf16[2,2,256,16,80]{4,2,3,0,1:T(8,128)(2,1)} async-done(((bf16[2,2,32,16,80]{4,2,3,0,1:T(8,128)(2,1)}), bf16[2,2,256,16,80]{4,2,3,0,1:T(8,128)(2,1)}) %all-gather.4.cloned.1.call-update) | async-done | bytes 2621456 | tf_op jit(solution)/shard_map/all_gather | solution.py:202
  91.9 2.4 fusion.89
  94.6 4.8 %fusion.318 = (f32[2,32]{1,0:T(2,128)S(1)}, f32[2,32,1280]{2,1,0:T(8,128)S(1)}) fusion(bf16[2,16,80,1280]{3,2,1,0:T(8,128)(2,1)} %param.24, bf16[2,2,256,16,80]{4,2,3,0,1:T(8,128)(2,1)} %all-gather.4.cloned.1.call-done, f32[2,16,32]{2,1,0:T(8,128)S(1)} %fusion.317, f32[2,16,32,256]{3,2,1,0:T(8,128)S(1)} %fusion.89, ...), kind=kOutput, calls=%fused_computation.338 | convolution fusion | flops 252937408 | bytes 7979264 | tf_op jit(solution)/shard_map/cqhk,hkd->cqd/dot_general | solution.py:206
  99.6 6.7 %fusion.204 = (u8[32,5120]{1,0:T(8,128)(4,1)S(1)}, u8[32,5120]{1,0:T(8,128)(4,1)S(1)}, f32[2,32,5120]{2,1,0:T(8,128)S(1)}) fusion(bf16[2,1280,5120]{2,1,0:T(8,128)(2,1)} %param.25, f32[2,32,1280]{2,1,0:T(8,128)S(1)} %get-tuple-element.30, f32[2,32]{1,0:T(2,128)S(1)} %add_rsqrt_fusion.4, f32[2,32]{1,0:T(2,128)S(1)} %broadcast_multiply_fusion.4), kind=kOutput, calls=%fused_computation.210 | convolution fusion | flops 843038720 | bytes 15073792 | tf_op jit(solution)/shard_map/cnd,df->cnf/dot_general | solution.py:207
  106.4 7.7 %fusion.319 = (f32[2,32]{1,0:T(2,128)S(1)}, f32[2,32,1280]{2,1,0:T(8,128)S(1)}) fusion(f32[2,32,1280]{2,1,0:T(8,128)S(1)} %get-tuple-element.30, bf16[2,5120,1280]{2,1,0:T(8,128)(2,1)} %param.26, f32[2,32,5120]{2,1,0:T(8,128)S(1)} %get-tuple-element.31, u8[32,5120]{1,0:T(8,128)(4,1)S(1)} %get-tuple-element.12, u8[32,5120]{1,0:T(8,128)(4,1)S(1)} %get-tuple-element.11), kind=kOutput, calls=%fused_computation.339 | convolution fusion | flops 862126016 | bytes 15401216 | tf_op jit(solution)/shard_map/cnf,fd->cnd/dot_general | solution.py:208
  114.4 4.1 %fusion.111 = bf16[3,2,32,16,80]{4,2,3,0,1:T(8,128)(2,1)S(1)} fusion(bf16[2,1280,3,16,80]{1,4,3,2,0:T(8,128)(2,1)S(1)} %bitcast.211, f32[2,32,1280]{2,1,0:T(8,128)S(1)} %get-tuple-element.33, f32[2,32]{1,0:T(2,128)S(1)} %add_rsqrt_fusion.3, f32[2,32]{1,0:T(2,128)S(1)} %broadcast_multiply_fusion.3), kind=kOutput, calls=%fused_computation.115 | convolution fusion | flops 629637120 | bytes 10651648 | tf_op jit(solution)/shard_map/cnd,dshk->scnhk/dot_general | solution.py:201
  119.4 4.2 %fusion.313 = (bf16[1,3,16,32,512]{4,3,2,1,0:T(8,128)(2,1)}, bf16[1,3,16,32,512]{4,3,2,1,0:T(8,128)(2,1)}) fusion(bf16[2,3,16,32,512]{4,3,2,1,0:T(8,128)(2,1)} %bitcast.206), kind=kLoop, calls=%fused_computation.333 | loop fusion | bytes 6291456 | tf_op jit(solution)/shard_map/slice | solution.py:250
  123.6 2.7 slice_bitcast_fusion.9
  127.3 2.3 slice_bitcast_fusion.8
  129.6 21.4 %all-gather.6.cloned.1.call-done = bf16[2,2,256,16,80]{4,2,3,0,1:T(8,128)(2,1)} async-done(((bf16[2,2,32,16,80]{4,2,3,0,1:T(8,128)(2,1)}), bf16[2,2,256,16,80]{4,2,3,0,1:T(8,128)(2,1)}) %all-gather.6.cloned.1.call-update) | async-done | bytes 2621456 | tf_op jit(solution)/shard_map/all_gather | solution.py:202
  151.0 2.4 fusion.90
  153.8 4.8 %fusion.321 = (f32[2,32]{1,0:T(2,128)S(1)}, f32[2,32,1280]{2,1,0:T(8,128)S(1)}) fusion(f32[2,32,1280]{2,1,0:T(8,128)S(1)} %get-tuple-element.33, bf16[2,16,80,1280]{3,2,1,0:T(8,128)(2,1)} %param.24, bf16[2,2,256,16,80]{4,2,3,0,1:T(8,128)(2,1)} %all-gather.6.cloned.1.call-done, f32[2,16,32]{2,1,0:T(8,128)S(1)} %fusion.320, f32[2,16,32,256]{3,2,1,0:T(8,128)S(1)} %fusion.90), kind=kOutput, calls=%fused_computation.341 | convolution fusion | flops 252855488 | bytes 8143104 | tf_op jit(solution)/shard_map/cqhk,hkd->cqd/dot_general | solution.py:206
  158.8 6.4 %fusion.205 = (u8[32,5120]{1,0:T(8,128)(4,1)S(1)}, u8[32,5120]{1,0:T(8,128)(4,1)S(1)}, f32[2,32,5120]{2,1,0:T(8,128)S(1)}) fusion(bf16[2,1280,5120]{2,1,0:T(8,128)(2,1)} %param.25, f32[2,32,1280]{2,1,0:T(8,128)S(1)} %get-tuple-element.35, f32[2,32]{1,0:T(2,128)S(1)} %add_rsqrt_fusion.2, f32[2,32]{1,0:T(2,128)S(1)} %broadcast_multiply_fusion.2), kind=kOutput, calls=%fused_computation.211 | convolution fusion | flops 843038720 | bytes 15073792 | tf_op jit(solution)/shard_map/cnd,df->cnf/dot_general | solution.py:207
  165.2 7.9 %fusion.322 = (f32[2,32]{1,0:T(2,128)S(1)}, f32[2,32,1280]{2,1,0:T(8,128)S(1)}) fusion(f32[2,32,1280]{2,1,0:T(8,128)S(1)} %get-tuple-element.35, bf16[2,5120,1280]{2,1,0:T(8,128)(2,1)} %param.26, f32[2,32,5120]{2,1,0:T(8,128)S(1)} %get-tuple-element.36, u8[32,5120]{1,0:T(8,128)(4,1)S(1)} %get-tuple-element.10, u8[32,5120]{1,0:T(8,128)(4,1)S(1)} %get-tuple-element.9), kind=kOutput, calls=%fused_computation.342 | convolution fusion | flops 862126016 | bytes 15401216 | tf_op jit(solution)/shard_map/cnf,fd->cnd/dot_general | solution.py:208
  173.7 2.3 collective-permute-start.2
  178.5 1.5 collective-permute-done.3
  181.8 34.0 %gather_rows.2.a_all = bf16[8,2,256,512]{3,2,1,0:T(8,128)(2,1)} custom-call(bf16[2,256,512]{2,1,0:T(8,128)(2,1)} %fusion.128.x_ref), custom_call_target="tpu_custom_call" | custom-call | tf_op jit(solution)/shard_map/gather_rows/pallas_call | solution.py:182
  215.8 39.6 %dec_first.1 = (bf16[2,256,512]{2,1,0:T(8,128)(2,1)}, bf16[2,256,512]{2,1,0:T(8,128)(2,1)}) custom-call(bf16[8,2,256,512]{3,2,1,0:T(8,128)(2,1)} %gather_rows.2.a_all, bf16[2,256,512]{2,1,0:T(8,128)(2,1)} %copy-done.2, bf16[1536,512]{1,0:T(8,128)(2,1)} %bitcast.204, bf16[512,512]{1,0:T(8,128)(2,1)} %bitcast.208, bf16[512,2048]{1,0:T(8,128)(2,1)} %get-tuple-element.18.wup, ...), custom_call_target="tpu_custom_call" | custom-call | tf_op jit(solution)/shard_map/dec_first/pallas_call | solution.py:132
  255.4 31.3 %gather_rows.3.a_all = bf16[8,2,256,512]{3,2,1,0:T(8,128)(2,1)} custom-call(bf16[2,256,512]{2,1,0:T(8,128)(2,1)} %get-tuple-element.7.x_ref), custom_call_target="tpu_custom_call" | custom-call | tf_op jit(solution)/shard_map/gather_rows/pallas_call | solution.py:182
  286.7 41.4 %dec_last.1 = f32[2,256,1536]{2,1,0:T(8,128)} custom-call(bf16[8,2,256,512]{3,2,1,0:T(8,128)(2,1)} %gather_rows.3.a_all, bf16[2,256,512]{2,1,0:T(8,128)(2,1)} %get-tuple-element.8.u_in, bf16[1536,512]{1,0:T(8,128)(2,1)} %bitcast.205, bf16[512,512]{1,0:T(8,128)(2,1)} %bitcast.207, bf16[512,2048]{1,0:T(8,128)(2,1)} %get-tuple-element.17.wup, ...), custom_call_target="tpu_custom_call" | custom-call | tf_op jit(solution)/shard_map/dec_last/pallas_call | solution.py:132
  (87 shorter events, 17.5 us)
Async XLA Ops:
  6.5 30.4 %copy-start = (bf16[2,256,1536]{2,1,0:T(8,128)(2,1)S(1)}, bf16[2,256,1536]{2,1,0:T(8,128)(2,1)}, u32[]{:S(2)}) copy-start(bf16[2,256,1536]{2,1,0:T(8,128)(2,1)} %param.17) | copy-start | bytes 4718596
  6.5 85.3 %all-gather.4.cloned.1.call-start = ((), (), s32[]{:S(2)}) async-start(), calls=%async_computation | async-start | bytes 4718592 | tf_op jit(solution)/shard_map/all_gather | solution.py:202
  36.9 3.3 copy-start.7
  40.5 2.6 collective-permute-start
  41.8 5.7 %collective-permute-start.1 = (bf16[2,16,1280]{2,1,0:T(8,128)(2,1)S(1)}, bf16[2,16,1280]{2,1,0:T(8,128)(2,1)S(1)}, u32[]{:S(2)}, u32[]{:S(2)}) collective-permute-start(bf16[2,16,1280]{2,1,0:T(8,128)(2,1)S(1)} %get-tuple-element.24), channel_id=1, source_target_pairs={{1,0},{2,1},{3,2},{4,3},{5,4},{6,5},{7,6}} | collective-permute-start | bytes 245768 | tf_op jit(solution)/shard_map/ppermute | solution.py:232
  56.6 94.4 %all-gather.6.cloned.1.call-start = ((), (), s32[]{:S(2)}) async-start(), calls=%async_computation.1 | async-start | bytes 4718592 | tf_op jit(solution)/shard_map/all_gather | solution.py:202
  99.6 14.7 %slice-start = ((s8[19660800]{0:T(1024)(128)(4,1)}), s8[4194304]{0:T(1024)(128)(4,1)S(1)}, s32[]{:S(2)}) async-start(s8[19660800]{0:T(1024)(128)(4,1)} %bitcast.210), calls=%async_computation.2 | async-start | bytes 8388608
  99.6 14.7 %slice-start.1 = ((s8[19660800]{0:T(1024)(128)(4,1)}), s8[4194304]{0:T(1024)(128)(4,1)S(1)}, s32[]{:S(2)}) async-start(s8[19660800]{0:T(1024)(128)(4,1)} %bitcast.210), calls=%async_computation.3 | async-start | bytes 8388608
  106.3 8.0 %slice-start.2 = ((s8[19660800]{0:T(1024)(128)(4,1)}), s8[4194304]{0:T(1024)(128)(4,1)S(1)}, s32[]{:S(2)}) async-start(s8[19660800]{0:T(1024)(128)(4,1)} %bitcast.210), calls=%async_computation.4 | async-start | bytes 8388608
  106.3 8.0 %slice-start.3 = ((s8[19660800]{0:T(1024)(128)(4,1)}), s8[4194304]{0:T(1024)(128)(4,1)S(1)}, s32[]{:S(2)}) async-start(s8[19660800]{0:T(1024)(128)(4,1)} %bitcast.210), calls=%async_computation.5 | async-start | bytes 8388608
  106.4 8.0 %slice-start.4 = ((s8[19660800]{0:T(1024)(128)(4,1)}), s8[2883584]{0:T(1024)(128)(4,1)S(1)}, s32[]{:S(2)}) async-start(s8[19660800]{0:T(1024)(128)(4,1)} %bitcast.210), calls=%async_computation.6 | async-start | bytes 5767168
  119.3 4.2 %copy-start.3 = (bf16[2,512,2048]{2,1,0:T(8,128)(2,1)S(1)}, bf16[2,512,2048]{2,1,0:T(8,128)(2,1)}, u32[]{:S(2)}) copy-start(bf16[2,512,2048]{2,1,0:T(8,128)(2,1)} %param.31) | copy-start | bytes 12582916
  123.6 3.7 %copy-start.4 = (bf16[2,2048,512]{2,1,0:T(8,128)(2,1)S(1)}, bf16[2,2048,512]{2,1,0:T(8,128)(2,1)}, u32[]{:S(2)}) copy-start(bf16[2,2048,512]{2,1,0:T(8,128)(2,1)} %param.32) | copy-start | bytes 12582916
  165.1 8.2 %copy-start.5 = (bf16[1280,512]{1,0:T(8,128)(2,1)S(1)}, bf16[1280,512]{1,0:T(8,128)(2,1)}, u32[]{:S(2)}) copy-start(bf16[1280,512]{1,0:T(8,128)(2,1)} %param.27) | copy-start | bytes 3932164
  173.1 4.3 %copy-start.6 = (bf16[2,16,32,512]{3,2,1,0:T(8,128)(2,1)S(1)}, bf16[2,16,32,512]{3,2,1,0:T(8,128)(2,1)}, u32[]{:S(2)}) copy-start(bf16[2,16,32,512]{3,2,1,0:T(8,128)(2,1)} %param.30) | copy-start | bytes 3145732
  173.7 4.7 %copy-start.9 = (bf16[512]{0:T(512)(128)(2,1)S(1)}, bf16[512]{0:T(512)(128)(2,1)}, u32[]{:S(2)}) copy-start(bf16[512]{0:T(512)(128)(2,1)} %param.28) | copy-start | bytes 3076
  173.7 4.7 %copy-start.8 = (bf16[256,512]{1,0:T(8,128)(2,1)S(1)}, bf16[256,512]{1,0:T(8,128)(2,1)}, u32[]{:S(2)}) copy-start(bf16[256,512]{1,0:T(8,128)(2,1)} %param.20) | copy-start | bytes 786436
  173.7 4.8 %collective-permute-start.2 = (bf16[2,16,512]{2,1,0:T(8,128)(2,1)S(1)}, bf16[2,16,512]{2,1,0:T(8,128)(2,1)S(1)}, u32[]{:S(2)}, u32[]{:S(2)}) collective-permute-start(bf16[2,16,512]{2,1,0:T(8,128)(2,1)S(1)} %get-tuple-element.25), channel_id=1, source_target_pairs={{0,1},{1,2},{2,3},{3,4},{4,5},{5,6},{6,7}} | collective-permute-start | bytes 98312 | tf_op jit(solution)/shard_map/ppermute | solution.py:237
  176.0 3.9 %collective-permute-start.3 = (bf16[2,16,512]{2,1,0:T(8,128)(2,1)S(1)}, bf16[2,16,512]{2,1,0:T(8,128)(2,1)S(1)}, u32[]{:S(2)}, u32[]{:S(2)}) collective-permute-start(bf16[2,16,512]{2,1,0:T(8,128)(2,1)S(1)} %get-tuple-element.26), channel_id=1, source_target_pairs={{1,0},{2,1},{3,2},{4,3},{5,4},{6,5},{7,6}} | collective-permute-start | bytes 98312 | tf_op jit(solution)/shard_map/ppermute | solution.py:238
  180.4 35.4 %copy-start.2 = (bf16[2,256,512]{2,1,0:T(8,128)(2,1)}, bf16[2,256,512]{2,1,0:T(8,128)(2,1)S(1)}, u32[]{:S(2)}) copy-start(bf16[2,256,512]{2,1,0:T(8,128)(2,1)S(1)} %get-tuple-element.40.u_in) | copy-start | bytes 1572868
  286.7 41.5 %copy-start.1 = (bf16[2,256,1536]{2,1,0:T(8,128)(2,1)S(1)}, bf16[2,256,1536]{2,1,0:T(8,128)(2,1)}, u32[]{:S(2)}) copy-start(bf16[2,256,1536]{2,1,0:T(8,128)(2,1)} %param.17) | copy-start | bytes 4718596
Sparse Core Ops, SparseCore 0:
  56.7 35.1 all-gather.3
  119.5 31.5 all-gather.5

commit v2 on v1

--- a/solution.py
+++ b/solution.py
@@ -8,6 +8,7 @@
 from jax.sharding import PartitionSpec as P
 
 KEEP_DIV = 8
+
 
 BF = jnp.bfloat16
 F32 = jnp.float32
@@ -190,64 +191,333 @@
     )(x)
 
 
-def layer_norm(hidden):
-    hid_f32 = hidden.astype(jnp.float32)
-    centred = hid_f32 - jnp.mean(hid_f32, axis=-1, keepdims=True)
-    row_var = jnp.mean(centred * centred, axis=-1, keepdims=True)
-    return (centred * lax.rsqrt(row_var + 1e-6)).astype(jnp.bfloat16)
-
-
-def attn_mlp_block(hidden, w_qkv, w_proj, w_up, w_down):
-    proj_qkv = jnp.einsum('cnd,dshk->scnhk', layer_norm(hidden), w_qkv, preferred_element_type=jnp.float32).astype(jnp.bfloat16)
-    kv_all = lax.all_gather(proj_qkv[1:], 'sp', axis=2, tiled=True)
-    scores = jnp.einsum('cqhk,cshk->chqs', proj_qkv[0], kv_all[0], preferred_element_type=jnp.float32) * proj_qkv.shape[-1] ** -0.5
-    attn_probs = jax.nn.softmax(scores, axis=-1).astype(jnp.bfloat16)
-    attended = jnp.einsum('chqs,cshk->cqhk', attn_probs, kv_all[1], preferred_element_type=jnp.float32).astype(jnp.bfloat16)
-    mid_state = (hidden + jnp.einsum('cqhk,hkd->cqd', attended, w_proj, preferred_element_type=jnp.float32)).astype(jnp.bfloat16)
-    up_act = jax.nn.gelu(jnp.einsum('cnd,df->cnf', layer_norm(mid_state), w_up, preferred_element_type=jnp.float32), approximate=False).astype(jnp.bfloat16)
-    return (mid_state + jnp.einsum('cnf,fd->cnd', up_act, w_down, preferred_element_type=jnp.float32)).astype(jnp.bfloat16)
+def enc_kernel(sp, mask_ref, patches_h, enc_pos_h, dec_pos_h, w_pe_h, b_pe_ref, qkv_h, proj_h, up_h, down_h, w_ed_h,
+               z_all, mask_all, pos_all,
+               patches, enc_pos, w_pe, w_ed, wbuf, e_src, win, edge, hid, a_all, qkv_s, s_s, p_s, o_s, g_s, acc_s,
+               wsem, insem, ms, mr, ws, wr, es, er, asend, arecv, zs, zr, pfs, pfr, pns, pnr, lsem):
+    me = lax.axis_index('sp')
+    n_clips, rows, width = patches.shape[0], patches.shape[1], hid.shape[1]
+    cap = e_src.shape[1]
+    share = cap // 2
+    half = share // 2
+    n_layers = qkv_h.shape[0]
+    my_rows = hid.shape[0]
+    per = sp // n_clips
+    heads = 16
+    hd = width // heads
+    clip = me // per
+    hf = lax.rem(me, 2)
+    partner = me + 1 - 2 * hf
+    my_half = me // per
+    slot = lax.rem(me, per)
+
+    def chunk(l, j):
+        if j < 3:
+            src = qkv_h.at[l, pl.ds(j * width, width), :]
+        elif j == 3:
+            src = proj_h.at[l]
+        elif j < 8:
+            src = up_h.at[l, :, pl.ds((j - 4) * width, width)]
+        else:
+            src = down_h.at[l, pl.ds((j - 8) * width, width), :]
+        return pltpu.make_async_copy(src, wbuf.at[j], wsem.at[j])
+
+    loads = [pltpu.make_async_copy(a, b, insem.at[i]) for i, (a, b) in enumerate(
+        [(patches_h, patches), (w_pe_h, w_pe), (enc_pos_h, enc_pos), (w_ed_h, w_ed)])]
+    for ld in loads:
+        ld.start()
+    for j in range(12):
+        chunk(0, j).start()
+
+    barrier = pltpu.get_barrier_semaphore()
+    for k in range(1, sp):
+        pl.semaphore_signal(barrier, inc=1, device_id={'sp': lax.rem(me + k, sp)}, device_id_type=MESH)
+    pl.semaphore_wait(barrier, sp - 1)
+
+    mask_sends = []
+    for k in range(1, sp):
+        mask_sends.append(pltpu.make_async_remote_copy(
+            src_ref=mask_ref, dst_ref=mask_all.at[me], send_sem=ms.at[k], recv_sem=mr.at[k],
+            device_id={'sp': lax.rem(me + k, sp)}, device_id_type=MESH))
+        mask_sends[-1].start()
+    own_mask = pltpu.make_async_copy(mask_ref, mask_all.at[me], lsem.at[0])
+    own_mask.start()
+
+    mask = mask_ref[...]
+    maskf = mask.astype(F32)
+    before = (lax.broadcasted_iota(jnp.int32, (rows, rows), 0) < lax.broadcasted_iota(jnp.int32, (rows, rows), 1))
+    mask8 = jnp.concatenate([maskf] + [jnp.zeros_like(maskf)] * 7, axis=0).astype(BF)
+    rank = mm(mask8, before.astype(BF)).astype(jnp.int32)
+    b_row = b_pe_ref[...].astype(F32)
+    row_id = lax.broadcasted_iota(jnp.int32, (cap, rows), 0)
+    for ld in loads[:3]:
+        ld.wait()
+    local = []
+    for c in range(n_clips):
+        pick = (row_id == rank[c:c + 1, :]) & (mask[c:c + 1, :] == 1)
+        pick = jnp.where(pick, 1.0, 0.0)
+        used = jnp.sum(pick, axis=1, keepdims=True)
+        pick = pick.astype(BF)
+        x = mm(pick, patches[c]).astype(BF)
+        pos = mm(pick, enc_pos[...])
+        local.append((mm(x, w_pe[...]) + used * b_row + pos).astype(BF))
+
+    for ms_ in mask_sends:
+        ms_.wait_recv()
+    own_mask.wait()
+    total_before = [jnp.zeros((1, rows), F32) for _ in range(n_clips)]
+    for s in range(sp):
+        ahead = jnp.where(s < me, 1.0, 0.0)
+        ms_row = mask_all[s].astype(F32)
+        for c in range(n_clips):
+            total_before[c] = total_before[c] + ahead * ms_row[c:c + 1, :]
+    sq0 = lax.broadcasted_iota(jnp.int32, (cap, cap), 0)
+    sq1 = lax.broadcasted_iota(jnp.int32, (cap, cap), 1)
+    for c in range(n_clips):
+        off = jnp.sum(total_before[c], axis=1, keepdims=True).astype(jnp.int32) - me * share + half
+        shift = jnp.where(sq0 == sq1 + off, 1.0, 0.0).astype(BF)
+        e_src[c] = mm(shift, local[c]).astype(BF)
+
+    def to(c, x, h):
+        return per * c + 2 * x + h
+
+    for c in range(n_clips):
+        for x in range(per // 2):
+            dst = to(c, x, my_half)
+
+            @pl.when(dst != me)
+            def _():
+                pltpu.make_async_remote_copy(
+                    src_ref=e_src.at[c], dst_ref=win.at[slot], send_sem=ws.at[c, x], recv_sem=wr.at[slot],
+                    device_id={'sp': dst}, device_id_type=MESH).start()
+
+            @pl.when(dst == me)
+            def _():
+                pltpu.make_async_copy(e_src.at[c], win.at[slot], wr.at[slot]).start()
+
+            for src_dev, h, r0 in ((per, 0, 0), (per - 1, 1, cap - half)):
+                edst = to(c, x, h)
+
+                @pl.when((me == src_dev) & (edst != me))
+                def _():
+                    pltpu.make_async_remote_copy(
+                        src_ref=e_src.at[c, pl.ds(r0, half)], dst_ref=edge, send_sem=es.at[c, x], recv_sem=er,
+                        device_id={'sp': edst}, device_id_type=MESH).start()
+
+                @pl.when((me == src_dev) & (edst == me))
+                def _():
+                    pltpu.make_async_copy(e_src.at[c, pl.ds(r0, half)], edge, er).start()
+
+    for b in range(per):
+        pltpu.make_async_copy(e_src.at[0], win.at[b], wr.at[b]).wait()
+    pltpu.make_async_copy(e_src.at[0, pl.ds(0, half)], edge, er).wait()
+
+    pos_own = pltpu.make_async_copy(dec_pos_h, pos_all.at[me], lsem.at[1])
+    pos_own.start()
+    pos_far = []
+    for k in range(1, sp // 2):
+        pos_far.append(pltpu.make_async_remote_copy(
+            src_ref=dec_pos_h, dst_ref=pos_all.at[me], send_sem=pfs.at[k], recv_sem=pfr.at[k],
+            device_id={'sp': lax.rem(me + 2 * k, sp)}, device_id_type=MESH))
+        pos_far[-1].start()
+
+    zero_edge = jnp.zeros((half, width), F32)
+    edge_v = edge[...].astype(F32)
+    first_prev = jnp.where(hf == 1, edge_v, zero_edge)
+    last_next = jnp.where(hf == 0, edge_v, zero_edge)
+    for b in range(per):
+        prev = first_prev if b == 0 else win[b - 1, cap - half:, :].astype(F32)
+        nxt = last_next if b == per - 1 else win[b + 1, :half, :].astype(F32)
+        lo = win[b, half:2 * half, :].astype(F32) + prev
+        hi = win[b, 2 * half:3 * half, :].astype(F32) + nxt
+        hid[b * share:b * share + half, :] = lo.astype(BF)
+        hid[b * share + half:(b + 1) * share, :] = hi.astype(BF)
+
+    scale = hd ** -0.5
+
+    def layer(l, carry):
+        def refill(j):
+            @pl.when(l < n_layers - 1)
+            def _():
+                chunk(l + 1, j).start()
+
+        a_all[l, 0] = norm_rows(hid[...])
+        swap = pltpu.make_async_remote_copy(
+            src_ref=a_all.at[l, 0], dst_ref=a_all.at[l, 1], send_sem=asend.at[l], recv_sem=arecv.at[l],
+            device_id={'sp': partner}, device_id_type=MESH)
+        swap.start()
+        swap.wait()
+        rhs = a_all[l].reshape(2 * my_rows, width)
+        for j in range(3):
+            chunk(l, j).wait()
+            qkv_s[j] = mm(wbuf[j], rhs, NT).astype(BF)
+            refill(j)
+        for h in range(heads):
+            s_s[h] = mm(qkv_s[0, h * hd:(h + 1) * hd, :my_rows], qkv_s[1, h * hd:(h + 1) * hd, :], TN)
+
+        def soft(i, cc):
+            s = s_s[i] * scale
+            e = jnp.exp(s - jnp.max(s, axis=-1, keepdims=True))
+            p_s[i] = (e / jnp.sum(e, axis=-1, keepdims=True)).astype(BF)
+            return cc
+
+        lax.fori_loop(0, heads, soft, 0, unroll=4)
+        for h in range(heads):
+            o_s[h * hd:(h + 1) * hd, :] = mm(qkv_s[2, h * hd:(h + 1) * hd, :], p_s[h], NT).astype(BF)
+        chunk(l, 3).wait()
+        h1 = (hid[...].astype(F32) + mm(o_s[...], wbuf[3], TN)).astype(BF)
+        hid[...] = h1
+        refill(3)
+        a2 = norm_rows(h1)
+        for j in range(4):
+            chunk(l, 4 + j).wait()
+            g_s[:, j * width:(j + 1) * width] = gelu(mm(a2, wbuf[4 + j])).astype(BF)
+            refill(4 + j)
+        for j in range(4):
+            chunk(l, 8 + j).wait()
+            part = mm(g_s[:, j * width:(j + 1) * width], wbuf[8 + j])
+            acc_s[...] = part if j == 0 else acc_s[...] + part
+            refill(8 + j)
+        hid[...] = (hid[...].astype(F32) + acc_s[...]).astype(BF)
+        return carry
+
+    lax.fori_loop(0, n_layers, layer, 0)
+
+    for p in pos_far:
+        p.wait()
+    pos_own.wait()
+    pos_near = []
+    for k in range(sp // 2):
+        piece = lax.rem(me + 2 * k, sp)
+        pos_near.append(pltpu.make_async_remote_copy(
+            src_ref=pos_all.at[piece], dst_ref=pos_all.at[piece], send_sem=pns.at[k], recv_sem=pnr.at[k],
+            device_id={'sp': partner}, device_id_type=MESH))
+        pos_near[-1].start()
+
+    loads[3].wait()
+    mine = z_all.at[clip, pl.ds(pl.multiple_of(hf * my_rows, my_rows), my_rows), :]
+    z_all[clip, pl.ds(pl.multiple_of(hf * my_rows, my_rows), my_rows), :] = mm(norm_rows(hid[...]), w_ed[...]).astype(BF)
+    z_sends = []
+    across = lax.rem(me + per, sp)
+    for i, dst in enumerate((across, across + 1 - 2 * hf, partner)):
+        z_sends.append(pltpu.make_async_remote_copy(
+            src_ref=mine, dst_ref=mine, send_sem=zs.at[i], recv_sem=zr.at[i],
+            device_id={'sp': dst}, device_id_type=MESH))
+        z_sends[-1].start()
+    for k in mask_sends:
+        k.wait_send()
+    for c in range(n_clips):
+        for x in range(per // 2):
+            @pl.when(to(c, x, my_half) != me)
+            def _():
+                pltpu.make_async_remote_copy(
+                    src_ref=e_src.at[c], dst_ref=win.at[slot], send_sem=ws.at[c, x], recv_sem=wr.at[slot],
+                    device_id={'sp': to(c, x, my_half)}, device_id_type=MESH).wait_send()
+
+            for src_dev, h, r0 in ((per, 0, 0), (per - 1, 1, cap - half)):
+                @pl.when((me == src_dev) & (to(c, x, h) != me))
+                def _():
+                    pltpu.make_async_remote_copy(
+                        src_ref=e_src.at[c, pl.ds(r0, half)], dst_ref=edge, send_sem=es.at[c, x], recv_sem=er,
+                        device_id={'sp': to(c, x, h)}, device_id_type=MESH).wait_send()
+    for p in pos_near:
+        p.wait()
+    for s in z_sends:
+        s.wait()
+
+
+def encode(sp, vis_mask, patches, enc_pos, dec_pos, w_pe, b_pe, qkv_t, proj, up, down, w_ed):
+    n_clips, rows, p_width = patches.shape
+    width = w_pe.shape[1]
+    d_width = w_ed.shape[1]
+    cap = 2 * rows // KEEP_DIV
+    my_rows = rows * sp // KEEP_DIV // 2
+    dma = pltpu.SemaphoreType.DMA
+    per = sp // n_clips
+    return pl.pallas_call(
+        functools.partial(enc_kernel, sp),
+        out_shape=(jax.ShapeDtypeStruct((n_clips, 2 * my_rows, d_width), BF),
+                   jax.ShapeDtypeStruct((sp, n_clips, rows), jnp.int32),
+                   jax.ShapeDtypeStruct((sp, rows, d_width), BF)),
+        in_specs=[VMEM, ANY, ANY, ANY, ANY, VMEM, ANY, ANY, ANY, ANY, ANY],
+        out_specs=(VMEM, VMEM, ANY),
+        scratch_shapes=[
+            pltpu.VMEM(patches.shape, BF), pltpu.VMEM(enc_pos.shape, BF), pltpu.VMEM(w_pe.shape, BF), pltpu.VMEM(w_ed.shape, BF),
+            pltpu.VMEM((12, width, width), BF),
+            pltpu.VMEM((n_clips, cap, width), BF), pltpu.VMEM((per, cap, width), BF), pltpu.VMEM((cap // 4, width), BF),
+            pltpu.VMEM((my_rows, width), BF), pltpu.VMEM((qkv_t.shape[0], 2, my_rows, width), BF),
+            pltpu.VMEM((3, width, 2 * my_rows), BF),
+            pltpu.VMEM((16, my_rows, 2 * my_rows), F32), pltpu.VMEM((16, my_rows, 2 * my_rows), BF),
+            pltpu.VMEM((width, my_rows), BF), pltpu.VMEM((my_rows, 4 * width), BF), pltpu.VMEM((my_rows, width), F32),
+            dma((12,)), dma((4,)), dma((sp,)), dma((sp,)), dma((n_clips, per // 2)), dma((per,)), dma((n_clips, per // 2)), dma,
+            dma((2,)), dma((2,)), dma((3,)), dma((3,)), dma((sp // 2,)), dma((sp // 2,)), dma((sp // 2,)), dma((sp // 2,)), dma((2,)),
+        ],
+        compiler_params=pltpu.CompilerParams(collective_id=1, has_side_effects=True, vmem_limit_bytes=62 << 20),
+        name='encode',
+    )(vis_mask, patches, enc_pos, dec_pos, w_pe, b_pe.reshape(1, width), qkv_t, proj, up, down, w_ed)
+
+
+def place_kernel(sp, z_ref, mask_all, pos_all, tok_ref, u_out, a_out, rank_s):
+    me = lax.axis_index('sp')
+    n_clips, n_vis, width = z_ref.shape
+    rows = mask_all.shape[2]
+    before = (lax.broadcasted_iota(jnp.int32, (rows, rows), 0) < lax.broadcasted_iota(jnp.int32, (rows, rows), 1)).astype(BF)
+    pad = 16
+    row_id = lax.broadcasted_iota(jnp.int32, (n_vis + pad, rows), 0)
+    for c in range(n_clips):
+        m = mask_all[:, c, :]
+        local = mm(m.astype(F32).astype(BF), before)
+        base = jnp.zeros((1, 1), F32)
+        for s in range(sp):
+            vis = m[s:s + 1, :]
+            rank = jnp.where(vis == 1, (local[s:s + 1, :] + base).astype(jnp.int32), n_vis)
+            base = base + jnp.sum(vis.astype(F32), axis=1, keepdims=True)
+            rank_s[c, s:s + 1, :] = rank
+        z_aug = jnp.concatenate([z_ref[c], tok_ref[...], jnp.zeros((pad - 1, width), BF)], axis=0)
+
+        def block(b, cc):
+            pick = jnp.where(row_id == rank_s[c, pl.ds(b, 1), :], 1.0, 0.0).astype(BF)
+            u = (mm(pick, z_aug, TN) + pos_all[b].astype(F32)).astype(BF)
+            a_out[b, c] = norm_rows(u)
+
+            @pl.when(b == me)
+            def _():
+                u_out[c] = u
+            return cc
+
+        lax.fori_loop(0, sp, block, 0)
+
+
+def place(sp, z_all, mask_all, pos_all, mask_token):
+    n_clips, n_vis, width = z_all.shape
+    rows = mask_all.shape[2]
+    return pl.pallas_call(
+        functools.partial(place_kernel, sp),
+        out_shape=(jax.ShapeDtypeStruct((n_clips, rows, width), BF), jax.ShapeDtypeStruct((sp, n_clips, rows, width), BF)),
+        in_specs=[VMEM] * 4,
+        out_specs=(VMEM, VMEM),
+        scratch_shapes=[pltpu.VMEM((n_clips, sp, rows), jnp.int32)],
+        name='place',
+    )(z_all, mask_all, pos_all, mask_token.reshape(1, width))
 
 
 def solution(mesh):
-    group_size = mesh.shape['sp']
-    to_next = [(src_dev, src_dev + 1) for src_dev in range(group_size - 1)]
-    to_prev = [(src_dev + 1, src_dev) for src_dev in range(group_size - 1)]
+    sp = mesh.shape['sp']
 
     def local_program(patches, vis_mask, enc_pos, dec_pos, w_pe, b_pe, enc_qkv, enc_proj, enc_up, enc_down, w_ed, mask_token, dec_qkv, dec_proj, dec_up, dec_down, w_out):
-        vis_shard = patches.shape[1] // KEEP_DIV
-        half_rows = vis_shard // 2
-        my_index = lax.axis_index('sp')
-        vis_counts = lax.all_gather(jnp.sum(vis_mask, axis=1), 'sp')
-        vis_before = jnp.sum(jnp.where(jnp.arange(group_size)[:, None] < my_index, vis_counts, 0), axis=0)
-        local_rank = jnp.cumsum(vis_mask, axis=1) - vis_mask
-        dest_row = vis_before[:, None] + local_rank - my_index * vis_shard + half_rows
-        row_ids = jnp.arange(2 * vis_shard)
-        select = ((dest_row[:, None, :] == row_ids[None, :, None]) & (vis_mask[:, None, :] == 1)).astype(jnp.bfloat16)
-        moved_x = jnp.einsum('cqi,cip->cqp', select, patches, preferred_element_type=jnp.float32).astype(jnp.bfloat16)
-        moved_pos = jnp.einsum('cqi,id->cqd', select, enc_pos, preferred_element_type=jnp.float32)
-        occupied = jnp.sum(select, axis=2, dtype=jnp.float32)
-        embedded = (jnp.einsum('cqp,pd->cqd', moved_x, w_pe, preferred_element_type=jnp.float32)
-                    + occupied[:, :, None] * b_pe.astype(jnp.float32) + moved_pos).astype(jnp.bfloat16)
-        from_prev = lax.ppermute(embedded[:, 3 * half_rows:], 'sp', to_next)
-        from_next = lax.ppermute(embedded[:, :half_rows], 'sp', to_prev)
-        hidden = embedded[:, half_rows:3 * half_rows] + jnp.concatenate([from_prev, from_next], axis=1)
-        for layer_idx in range(enc_qkv.shape[0]):
-            hidden = attn_mlp_block(hidden, enc_qkv[layer_idx], enc_proj[layer_idx], enc_up[layer_idx], enc_down[layer_idx])
-        z_enc = jnp.einsum('cnd,de->cne', layer_norm(hidden), w_ed, preferred_element_type=jnp.float32).astype(jnp.bfloat16)
-        z_prev = lax.ppermute(z_enc[:, half_rows:], 'sp', to_next)
-        z_next = lax.ppermute(z_enc[:, :half_rows], 'sp', to_prev)
-        z_rows = jnp.concatenate([z_prev, z_enc, z_next], axis=1)
-        placed = jnp.einsum('cqi,cqe->cie', select, z_rows, preferred_element_type=jnp.float32)
-        masked_part = (1 - vis_mask).astype(jnp.float32)[:, :, None] * mask_token.astype(jnp.float32)
-        hidden = (placed + masked_part + dec_pos.astype(jnp.float32)).astype(jnp.bfloat16)
-        n_layers, d_width = dec_qkv.shape[:2]
-        wqkv_t = jnp.transpose(dec_qkv, (0, 2, 3, 4, 1)).reshape(n_layers, 3 * d_width, d_width)
+        n_layers, width = enc_qkv.shape[:2]
+        d_width = dec_qkv.shape[1]
+        enc_qkv_t = jnp.transpose(enc_qkv, (0, 2, 3, 4, 1)).reshape(n_layers, 3 * width, width)
+        dec_qkv_t = jnp.transpose(dec_qkv, (0, 2, 3, 4, 1)).reshape(n_layers, 3 * d_width, d_width)
+        z_all, mask_all, pos_all = encode(sp, vis_mask, patches, enc_pos, dec_pos, w_pe, b_pe, enc_qkv_t,
+                                          enc_proj.reshape(n_layers, width, width), enc_up, enc_down, w_ed)
+        hidden, a_all = place(sp, z_all, mask_all, pos_all, mask_token)
         wproj = dec_proj.reshape(n_layers, d_width, d_width)
-        acts = layer_norm(hidden)
         for layer_idx in range(n_layers):
             last = layer_idx == n_layers - 1
-            a_all = gather(group_size, acts)
-            res = dec_layer(last, group_size, a_all, hidden, wqkv_t[layer_idx], wproj[layer_idx], dec_up[layer_idx], dec_down[layer_idx], w_out)
+            if layer_idx:
+                a_all = gather(sp, acts)
+            res = dec_layer(last, sp, a_all, hidden, dec_qkv_t[layer_idx], wproj[layer_idx], dec_up[layer_idx], dec_down[layer_idx], w_out)
             if not last:
                 hidden, acts = res
         return res

time: 336 us -> 206 us (0.61)
  waiting for transfers between devices: 62.5 us -> 0 us
  matrix products: 59.5 us -> 0 us
  Pallas kernels: 146 us -> 191 us
  blocking collectives: 25 us -> 0 us
  between operations: 13.8 us -> 0.02 us
  other arithmetic: 7.33 us -> 0 us
  starting transfers between devices: 6.21 us -> 0 us
    pallas_call x0 -> x2, Pallas kernels: none -> 79 us  [the longest x1 66.6 us: encode(): pl.pallas_call(functools.partial(enc_kernel, sp), out_shape=(jax.ShapeDty...]
    dot_general x14 -> x0, matrix products: 59.5 us -> none  [the longest x2 15.7 us: attn_mlp_block(): jnp.einsum('cnf,fd->cnd', up_act, w_down, preferred_element_type=jnp.floa...]
    all_gather x2 -> x0, waiting for transfers between devices: 56.7 us -> none  [attn_mlp_block(): kv_all = lax.all_gather(proj_qkv[1:], 'sp', axis=2, tiled=True)]
    pallas_call x2 -> x1, Pallas kernels: 65.3 us -> 30.8 us  [gather(): pl.pallas_call(functools.partial(gather_kernel, sp), out_shape=jax.ShapeD...]
    unnamed x1 -> x0, blocking collectives: 25 us -> none
    ppermute x4 -> x0, starting transfers between devices: 6.17 us -> none  [the longest x1 2.29 us: local_program(): z_prev = lax.ppermute(z_enc[:, half_rows:], 'sp', to_next)]
    ppermute x4 -> x0, waiting for transfers between devices: 5.83 us -> none  [the longest x1 4.37 us: local_program(): from_next = lax.ppermute(embedded[:, :half_rows], 'sp', to_prev)]
  transfers between devices with their start and end apart: 6 -> 0, of which waited for: 4 -> 0; matrix products, arithmetic and copies ran while one was open for 3% -> 0% of each run, Pallas kernels for 0% -> 0%
where the time goes in v2:
time: 206 us
  Pallas kernels  191 us (93%)
  local copies, waits for them, and re-layouts  15 us (7%)
    pallas_call x2, Pallas kernels, dec_layer(): pl.pallas_call(functools.partial(dec_kernel, last, n_clips, sp), out_shap...  81 us
    pallas_call x1, Pallas kernels, encode(): pl.pallas_call(functools.partial(enc_kernel, sp), out_shape=(jax.ShapeDty...  66.6 us
    pallas_call x1, Pallas kernels, gather(): pl.pallas_call(functools.partial(gather_kernel, sp), out_shape=jax.ShapeD...  30.8 us
    pallas_call x1, Pallas kernels, place(): pl.pallas_call(functools.partial(place_kernel, sp), out_shape=(jax.ShapeD...  12.4 us
    slice x1, local copies, waits for them, and re-layouts, local_program(): dec_qkv_t[layer_idx]  4.2 us

profile of v2, /device:TPU:0, one launch (start us, length us, event | category | flops | bytes accessed | tf_op | source)
XLA Modules:
  0.0 205.8 jit_solution(13665734475009522788)
XLA Ops:
  0.0 1.3 reshape.25.tok_ref
  1.3 1.3 reshape.22.b_pe_ref
  2.5 2.3 %fusion.1 = (bf16[1,16,32,512]{3,2,1,0:T(8,128)(2,1)}, bf16[1,16,32,512]{3,2,1,0:T(8,128)(2,1)}) fusion(bf16[2,16,32,512]{3,2,1,0:T(8,128)(2,1)} %param.30), kind=kLoop, calls=%fused_computation.5 | loop fusion | bytes 2097152 | tf_op jit(solution)/shard_map/slice | solution.py:520
  4.8 66.6 %encode.1 = (bf16[2,256,512]{2,1,0:T(8,128)(2,1)}, s32[8,2,256]{2,1,0:T(2,128)}, bf16[8,256,512]{2,1,0:T(8,128)(2,1)}) custom-call(s32[2,256]{1,0:T(2,128)} %mask_ref.1, bf16[2,256,1536]{2,1,0:T(8,128)(2,1)} %patches_h.1, bf16[256,1280]{1,0:T(8,128)(2,1)} %enc_pos_h.1, bf16[256,512]{1,0:T(8,128)(2,1)} %dec_pos_h.1, bf16[1536,1280]{1,0:T(8,128)(2,1)} %w_pe_h.1, ...), custom_call_target="tpu_custom_call" | custom-call | tf_op jit(solution)/shard_map/encode/pallas_call | solution.py:437
  71.4 12.4 %place.1 = (bf16[2,256,512]{2,1,0:T(8,128)(2,1)}, bf16[8,2,256,512]{3,2,1,0:T(8,128)(2,1)}) custom-call(bf16[2,256,512]{2,1,0:T(8,128)(2,1)} %get-tuple-element.12.z_ref, s32[8,2,256]{2,1,0:T(2,128)} %get-tuple-element.13.mask_all, bf16[8,256,512]{2,1,0:T(8,128)(2,1)} %get-tuple-element.14.pos_all, bf16[1,512]{1,0:T(2,128)(2,1)} %reshape.25.tok_ref), custom_call_target="tpu_custom_call" | custom-call | tf_op jit(solution)/shard_map/place/pallas_call | solution.py:494
  83.8 0.0 copy-start
  83.8 4.2 %fusion = (bf16[1,3,16,32,512]{4,3,2,1,0:T(8,128)(2,1)}, bf16[1,3,16,32,512]{4,3,2,1,0:T(8,128)(2,1)}) fusion(bf16[2,3,16,32,512]{4,3,2,1,0:T(8,128)(2,1)} %bitcast.21), kind=kLoop, calls=%fused_computation.4 | loop fusion | bytes 6291456 | tf_op jit(solution)/shard_map/slice | solution.py:520
  88.0 0.0 copy-done
  88.0 0.0 copy-start.1
  88.0 2.7 %slice_bitcast_fusion.1 = (bf16[512,2048]{1,0:T(8,128)(2,1)}, bf16[512,2048]{1,0:T(8,128)(2,1)}) fusion(bf16[2,512,2048]{2,1,0:T(8,128)(2,1)S(1)} %copy-done), kind=kLoop, calls=%fused_computation.1 | loop fusion | bytes 8388608 | tf_op jit(solution)/shard_map/squeeze | solution.py:520
  90.7 1.0 copy-done.1
  91.7 2.3 %slice_bitcast_fusion = (bf16[2048,512]{1,0:T(8,128)(2,1)}, bf16[2048,512]{1,0:T(8,128)(2,1)}) fusion(bf16[2,2048,512]{2,1,0:T(8,128)(2,1)S(1)} %copy-done.1), kind=kLoop, calls=%fused_computation | loop fusion | bytes 8388608 | tf_op jit(solution)/shard_map/squeeze | solution.py:520
  94.0 39.6 %dec_first.1 = (bf16[2,256,512]{2,1,0:T(8,128)(2,1)}, bf16[2,256,512]{2,1,0:T(8,128)(2,1)}) custom-call(bf16[8,2,256,512]{3,2,1,0:T(8,128)(2,1)} %get-tuple-element.15.a_all, bf16[2,256,512]{2,1,0:T(8,128)(2,1)} %get-tuple-element.16.u_in, bf16[1536,512]{1,0:T(8,128)(2,1)} %bitcast.19, bf16[512,512]{1,0:T(8,128)(2,1)} %bitcast.23, ...), custom_call_target="tpu_custom_call" | custom-call | tf_op jit(solution)/shard_map/dec_first/pallas_call | solution.py:133
  133.7 30.8 %gather_rows.1.a_all = bf16[8,2,256,512]{3,2,1,0:T(8,128)(2,1)} custom-call(bf16[2,256,512]{2,1,0:T(8,128)(2,1)} %get-tuple-element.17.x_ref), custom_call_target="tpu_custom_call" | custom-call | tf_op jit(solution)/shard_map/gather_rows/pallas_call | solution.py:183
  164.4 41.3 %dec_last.1 = f32[2,256,1536]{2,1,0:T(8,128)} custom-call(bf16[8,2,256,512]{3,2,1,0:T(8,128)(2,1)} %gather_rows.1.a_all, bf16[2,256,512]{2,1,0:T(8,128)(2,1)} %get-tuple-element.18.u_in, bf16[1536,512]{1,0:T(8,128)(2,1)} %bitcast.20, bf16[512,512]{1,0:T(8,128)(2,1)} %bitcast.22, bf16[512,2048]{1,0:T(8,128)(2,1)} %get-tuple-element.21.wup, ...), custom_call_target="tpu_custom_call" | custom-call | tf_op jit(solution)/shard_map/dec_last/pallas_call | solution.py:133
Async XLA Ops:
  83.8 4.2 %copy-start = (bf16[2,512,2048]{2,1,0:T(8,128)(2,1)S(1)}, bf16[2,512,2048]{2,1,0:T(8,128)(2,1)}, u32[]{:S(2)}) copy-start(bf16[2,512,2048]{2,1,0:T(8,128)(2,1)} %param.31) | copy-start | bytes 12582916
  88.0 3.7 %copy-start.1 = (bf16[2,2048,512]{2,1,0:T(8,128)(2,1)S(1)}, bf16[2,2048,512]{2,1,0:T(8,128)(2,1)}, u32[]{:S(2)}) copy-start(bf16[2,2048,512]{2,1,0:T(8,128)(2,1)} %param.32) | copy-start | bytes 12582916

commit v3 on v2

--- a/solution.py
+++ b/solution.py
@@ -83,112 +83,6 @@
         return nxt
 
     lax.fori_loop(0, heads // 2, body, first)
-
-
-def dec_kernel(last, n_clips, sp, a_all, u_in, wqkv, wproj, wup, wdown, wout, *rest):
-    if last:
-        out, k_s, vt_s, q_s, s_s, o_s = rest
-    else:
-        out, a_out, k_s, vt_s, q_s, s_s, o_s = rest
-    rows = u_in.shape[1]
-    width = u_in.shape[2]
-    tok = rows * sp
-    heads, hd = 16, width // 16
-    me = lax.axis_index('sp')
-
-    def clip(c, carry):
-        def kv(b, cc):
-            at = pl.multiple_of(b * rows, rows)
-            blk = a_all[b, c]
-            k_s[pl.ds(at, rows), :] = mm(blk, wqkv[width:2 * width, :], NT).astype(BF)
-            vt_s[:, pl.ds(at, rows)] = mm(wqkv[2 * width:, :], blk, NT).astype(BF)
-            return cc
-
-        lax.fori_loop(0, sp, kv, 0)
-        q_s[...] = mm(wqkv[:width, :], a_all[me, c], NT).astype(BF)
-        attend_clip(tok, rows, heads, hd, k_s, vt_s, q_s, s_s, o_s)
-        h1 = (u_in[c].astype(F32) + mm(o_s[...], wproj[...], TN)).astype(BF)
-        g = gelu(mm(norm_rows(h1), wup[...])).astype(BF)
-        u2 = (h1.astype(F32) + mm(g, wdown[...])).astype(BF)
-        a2 = norm_rows(u2)
-        if last:
-            out[c] = mm(a2, wout[...])
-        else:
-            out[c] = u2
-            a_out[c] = a2
-        return carry
-
-    lax.fori_loop(0, n_clips, clip, 0)
-
-
-def dec_layer(last, sp, a_all, u_in, wqkv, wproj, wup, wdown, wout):
-    n_clips, rows, width = u_in.shape
-    tok = rows * sp
-    if last:
-        shape = jax.ShapeDtypeStruct((n_clips, rows, wout.shape[1]), F32)
-        specs = VMEM
-    else:
-        shape = (jax.ShapeDtypeStruct(u_in.shape, BF),) * 2
-        specs = (VMEM, VMEM)
-    return pl.pallas_call(
-        functools.partial(dec_kernel, last, n_clips, sp),
-        out_shape=shape,
-        in_specs=[VMEM] * 7,
-        out_specs=specs,
-        scratch_shapes=[
-            pltpu.VMEM((tok, width), BF),
-            pltpu.VMEM((width, tok), BF),
-            pltpu.VMEM((width, rows), BF),
-            pltpu.VMEM((2, tok, rows), F32),
-            pltpu.VMEM((width, rows), BF),
-        ],
-        compiler_params=pltpu.CompilerParams(vmem_limit_bytes=60 << 20),
-        name='dec_last' if last else 'dec_first',
-    )(a_all, u_in, wqkv, wproj, wup, wdown, wout)
-
-
-def gather_kernel(sp, x_ref, all_ref, send_a, recv_a, send_b, recv_b, loc):
-    me = lax.axis_index('sp')
-    partner = me + 1 - 2 * lax.rem(me, 2)
-    barrier = pltpu.get_barrier_semaphore()
-    for k in range(1, sp):
-        pl.semaphore_signal(barrier, inc=1, device_id={'sp': lax.rem(me + k, sp)}, device_id_type=MESH)
-    pl.semaphore_wait(barrier, sp - 1)
-    own = pltpu.make_async_copy(x_ref, all_ref.at[me], loc)
-    own.start()
-    far = []
-    near = []
-    for k in range(sp // 2):
-        near.append(pltpu.make_async_remote_copy(
-            src_ref=x_ref if k == 0 else all_ref.at[lax.rem(me + sp - 2 * k, sp)],
-            dst_ref=all_ref.at[lax.rem(me + sp - 2 * k, sp)],
-            send_sem=send_b.at[k], recv_sem=recv_b.at[k], device_id={'sp': partner}, device_id_type=MESH))
-        if k:
-            far.append(pltpu.make_async_remote_copy(
-                src_ref=x_ref, dst_ref=all_ref.at[me], send_sem=send_a.at[k], recv_sem=recv_a.at[k],
-                device_id={'sp': lax.rem(me + 2 * k, sp)}, device_id_type=MESH))
-            far[-1].start()
-    near[0].start()
-    for k in range(1, sp // 2):
-        far[k - 1].wait_recv()
-        near[k].start()
-    for k in range(sp // 2):
-        near[k].wait()
-    for f in far:
-        f.wait_send()
-    own.wait()
-
-
-def gather(sp, x):
-    return pl.pallas_call(
-        functools.partial(gather_kernel, sp),
-        out_shape=jax.ShapeDtypeStruct((sp,) + x.shape, x.dtype),
-        in_specs=[VMEM],
-        out_specs=VMEM,
-        scratch_shapes=[pltpu.SemaphoreType.DMA((sp // 2,))] * 4 + [pltpu.SemaphoreType.DMA],
-        compiler_params=pltpu.CompilerParams(collective_id=0, has_side_effects=True),
-        name='gather_rows',
-    )(x)
 
 
 def enc_kernel(sp, mask_ref, patches_h, enc_pos_h, dec_pos_h, w_pe_h, b_pe_ref, qkv_h, proj_h, up_h, down_h, w_ed_h,
@@ -248,7 +142,7 @@
     before = (lax.broadcasted_iota(jnp.int32, (rows, rows), 0) < lax.broadcasted_iota(jnp.int32, (rows, rows), 1))
     mask8 = jnp.concatenate([maskf] + [jnp.zeros_like(maskf)] * 7, axis=0).astype(BF)
     rank = mm(mask8, before.astype(BF)).astype(jnp.int32)
-    b_row = b_pe_ref[...].astype(F32)
+    b_row = b_pe_ref[...].reshape(1, width).astype(F32)
     row_id = lax.broadcasted_iota(jnp.int32, (cap, rows), 0)
     for ld in loads[:3]:
         ld.wait()
@@ -454,13 +348,29 @@
         ],
         compiler_params=pltpu.CompilerParams(collective_id=1, has_side_effects=True, vmem_limit_bytes=62 << 20),
         name='encode',
-    )(vis_mask, patches, enc_pos, dec_pos, w_pe, b_pe.reshape(1, width), qkv_t, proj, up, down, w_ed)
-
-
-def place_kernel(sp, z_ref, mask_all, pos_all, tok_ref, u_out, a_out, rank_s):
+    )(vis_mask, patches, enc_pos, dec_pos, w_pe, b_pe, qkv_t, proj, up, down, w_ed)
+
+
+def decode_kernel(sp, z_ref, mask_all, pos_h, tok_ref, wqkv_h, wproj_h, wup_h, wdown_h, a_out,
+                  pos, wqkv, wproj, wup, wdown, rank_s, u_s, a_own, a_all, k_s, vt_s, q_s, s_s, o_s,
+                  insem, fs, fr, ns, nr):
     me = lax.axis_index('sp')
+    partner = me + 1 - 2 * lax.rem(me, 2)
     n_clips, n_vis, width = z_ref.shape
     rows = mask_all.shape[2]
+    tok = rows * sp
+    heads, hd = 16, width // 16
+    n_far = sp // 2
+
+    loads = [pltpu.make_async_copy(a, b, insem.at[i]) for i, (a, b) in enumerate(
+        [(pos_h, pos), (wqkv_h, wqkv), (wproj_h, wproj), (wup_h, wup), (wdown_h, wdown)])]
+    for ld in loads:
+        ld.start()
+    barrier = pltpu.get_barrier_semaphore()
+    for k in range(1, sp):
+        pl.semaphore_signal(barrier, inc=1, device_id={'sp': lax.rem(me + k, sp)}, device_id_type=MESH)
+    pl.semaphore_wait(barrier, sp - 1)
+
     before = (lax.broadcasted_iota(jnp.int32, (rows, rows), 0) < lax.broadcasted_iota(jnp.int32, (rows, rows), 1)).astype(BF)
     pad = 16
     row_id = lax.broadcasted_iota(jnp.int32, (n_vis + pad, rows), 0)
@@ -470,35 +380,129 @@
         base = jnp.zeros((1, 1), F32)
         for s in range(sp):
             vis = m[s:s + 1, :]
-            rank = jnp.where(vis == 1, (local[s:s + 1, :] + base).astype(jnp.int32), n_vis)
+            rank_s[c, s:s + 1, :] = jnp.where(vis == 1, (local[s:s + 1, :] + base).astype(jnp.int32), n_vis)
             base = base + jnp.sum(vis.astype(F32), axis=1, keepdims=True)
-            rank_s[c, s:s + 1, :] = rank
-        z_aug = jnp.concatenate([z_ref[c], tok_ref[...], jnp.zeros((pad - 1, width), BF)], axis=0)
+    for ld in loads:
+        ld.wait()
+
+    def far(c, k):
+        return pltpu.make_async_remote_copy(
+            src_ref=a_own.at[c], dst_ref=a_all.at[c, me], send_sem=fs.at[c, k], recv_sem=fr.at[c, k],
+            device_id={'sp': lax.rem(me + 2 * k, sp)}, device_id_type=MESH)
+
+    def near(c, k):
+        piece = lax.rem(me + 2 * k, sp)
+        return pltpu.make_async_remote_copy(
+            src_ref=a_all.at[c, piece] if k else a_own.at[c], dst_ref=a_all.at[c, piece],
+            send_sem=ns.at[c, k], recv_sem=nr.at[c, k], device_id={'sp': partner}, device_id_type=MESH)
+
+    def relay(c):
+        for k in range(1, n_far):
+            far(c, k).wait_recv()
+        for k in range(n_far):
+            near(c, k).start()
+
+    def keys_values(l, b, blk):
+        at = pl.multiple_of(b * rows, rows)
+        k_s[pl.ds(at, rows), :] = mm(blk, wqkv[l, width:2 * width, :], NT).astype(BF)
+        vt_s[:, pl.ds(at, rows)] = mm(wqkv[l, 2 * width:, :], blk, NT).astype(BF)
+
+    def attend(l, c):
+        q_s[...] = mm(wqkv[l, :width, :], a_own[c], NT).astype(BF)
+        attend_clip(tok, rows, heads, hd, k_s, vt_s, q_s, s_s, o_s)
+
+    def feed(l, c):
+        h1 = (u_s[c].astype(F32) + mm(o_s[...], wproj[l], TN)).astype(BF)
+        g = gelu(mm(norm_rows(h1), wup[l])).astype(BF)
+        return (h1.astype(F32) + mm(g, wdown[l])).astype(BF)
+
+    def first(c, carry):
+        z_aug = jnp.concatenate([z_ref[c], tok_ref[...].reshape(1, width), jnp.zeros((pad - 1, width), BF)], axis=0)
 
         def block(b, cc):
             pick = jnp.where(row_id == rank_s[c, pl.ds(b, 1), :], 1.0, 0.0).astype(BF)
-            u = (mm(pick, z_aug, TN) + pos_all[b].astype(F32)).astype(BF)
-            a_out[b, c] = norm_rows(u)
+            u = (mm(pick, z_aug, TN) + pos[b].astype(F32)).astype(BF)
+            a = norm_rows(u)
+            keys_values(0, b, a)
 
             @pl.when(b == me)
             def _():
-                u_out[c] = u
+                u_s[c] = u
+                a_own[c] = a
             return cc
 
         lax.fori_loop(0, sp, block, 0)
-
-
-def place(sp, z_all, mask_all, pos_all, mask_token):
+        attend(0, c)
+
+        @pl.when(c == 1)
+        def _():
+            relay(0)
+
+        u1 = feed(0, c)
+        u_s[c] = u1
+        a_own[c] = norm_rows(u1)
+        for k in range(1, n_far):
+            far(c, k).start()
+        return carry
+
+    lax.fori_loop(0, n_clips, first, 0)
+
+    def second(c, carry):
+        keys_values(1, me, a_own[c])
+
+        def same(k, cc):
+            b = lax.rem(me + 2 * k, sp)
+            keys_values(1, b, a_all[c, b])
+            return cc
+
+        def other(k, cc):
+            b = lax.rem(partner + 2 * k, sp)
+            keys_values(1, b, a_all[c, b])
+            return cc
+
+        lax.fori_loop(1, n_far, same, 0)
+        for k in range(n_far):
+            near(c, k).wait_recv()
+        lax.fori_loop(0, n_far, other, 0)
+        attend(1, c)
+
+        @pl.when(c == 0)
+        def _():
+            relay(1)
+
+        a_out[c] = norm_rows(feed(1, c))
+        return carry
+
+    lax.fori_loop(0, n_clips, second, 0)
+    for c in range(n_clips):
+        for k in range(n_far):
+            near(c, k).wait_send()
+            if k:
+                far(c, k).wait_send()
+
+
+def decode(sp, z_all, mask_all, pos_all, mask_token, wqkv, wproj, wup, wdown):
     n_clips, n_vis, width = z_all.shape
     rows = mask_all.shape[2]
+    tok = rows * sp
+    dma = pltpu.SemaphoreType.DMA
     return pl.pallas_call(
-        functools.partial(place_kernel, sp),
-        out_shape=(jax.ShapeDtypeStruct((n_clips, rows, width), BF), jax.ShapeDtypeStruct((sp, n_clips, rows, width), BF)),
-        in_specs=[VMEM] * 4,
-        out_specs=(VMEM, VMEM),
-        scratch_shapes=[pltpu.VMEM((n_clips, sp, rows), jnp.int32)],
-        name='place',
-    )(z_all, mask_all, pos_all, mask_token.reshape(1, width))
+        functools.partial(decode_kernel, sp),
+        out_shape=jax.ShapeDtypeStruct((n_clips, rows, width), BF),
+        in_specs=[VMEM, VMEM, ANY, VMEM, ANY, ANY, ANY, ANY],
+        out_specs=VMEM,
+        scratch_shapes=[
+            pltpu.VMEM(pos_all.shape, BF), pltpu.VMEM(wqkv.shape, BF), pltpu.VMEM(wproj.shape, BF),
+            pltpu.VMEM(wup.shape, BF), pltpu.VMEM(wdown.shape, BF),
+            pltpu.VMEM((n_clips, sp, rows), jnp.int32), pltpu.VMEM((n_clips, rows, width), BF), pltpu.VMEM((n_clips, rows, width), BF),
+            pltpu.VMEM((n_clips, sp, rows, width), BF),
+            pltpu.VMEM((tok, width), BF), pltpu.VMEM((width, tok), BF), pltpu.VMEM((width, rows), BF),
+            pltpu.VMEM((2, tok, rows), F32), pltpu.VMEM((width, rows), BF),
+            dma((5,)), dma((n_clips, sp // 2)), dma((n_clips, sp // 2)), dma((n_clips, sp // 2)), dma((n_clips, sp // 2)),
+        ],
+        compiler_params=pltpu.CompilerParams(collective_id=2, has_side_effects=True, vmem_limit_bytes=52 << 20),
+        name='decode',
+    )(z_all, mask_all, pos_all, mask_token, wqkv, wproj, wup, wdown)
 
 
 def solution(mesh):
@@ -511,16 +515,9 @@
         dec_qkv_t = jnp.transpose(dec_qkv, (0, 2, 3, 4, 1)).reshape(n_layers, 3 * d_width, d_width)
         z_all, mask_all, pos_all = encode(sp, vis_mask, patches, enc_pos, dec_pos, w_pe, b_pe, enc_qkv_t,
                                           enc_proj.reshape(n_layers, width, width), enc_up, enc_down, w_ed)
-        hidden, a_all = place(sp, z_all, mask_all, pos_all, mask_token)
-        wproj = dec_proj.reshape(n_layers, d_width, d_width)
-        for layer_idx in range(n_layers):
-            last = layer_idx == n_layers - 1
-            if layer_idx:
-                a_all = gather(sp, acts)
-            res = dec_layer(last, sp, a_all, hidden, dec_qkv_t[layer_idx], wproj[layer_idx], dec_up[layer_idx], dec_down[layer_idx], w_out)
-            if not last:
-                hidden, acts = res
-        return res
+        acts = decode(sp, z_all, mask_all, pos_all, mask_token, dec_qkv_t,
+                      dec_proj.reshape(n_layers, d_width, d_width), dec_up, dec_down)
+        return jnp.einsum('cne,ep->cnp', acts, w_out, preferred_element_type=F32)
 
     row_spec = P('dp', 'sp', None)
     pos_spec = P(('dp', 'sp'), None)

time: 206 us -> 152 us (0.74)
  Pallas kernels: 191 us -> 147 us
  local copies, waits for them, and re-layouts: 15 us -> 1.76 us
  matrix products: 0 us -> 2.65 us
    pallas_call x4 -> x1, Pallas kernels: 124 us -> 80.8 us  [decode(): pl.pallas_call(functools.partial(decode_kernel, sp), out_shape=jax.ShapeD...]
    slice x2 -> x0, local copies, waits for them, and re-layouts: 6.49 us -> none  [the longest x1 4.2 us: local_program(): dec_qkv_t[layer_idx]]
    squeeze x2 -> x0, local copies, waits for them, and re-layouts: 4.96 us -> none  [the longest x1 2.66 us: local_program(): dec_up[layer_idx]]
    dot_general x0 -> x1, matrix products: none -> 2.65 us  [local_program(): return jnp.einsum('cne,ep->cnp', acts, w_out, preferred_element_type=F32)]
    reshape x2 -> x0, local copies, waits for them, and re-layouts: 2.54 us -> none  [the longest x1 1.28 us: encode(): b_pe.reshape(1, width)]
where the time goes in v3:
time: 152 us
  Pallas kernels  147 us (97%)
  matrix products  2.65 us (2%)
  local copies, waits for them, and re-layouts  1.76 us (1%)
    pallas_call x1, Pallas kernels, decode(): pl.pallas_call(functools.partial(decode_kernel, sp), out_shape=jax.ShapeD...  80.8 us
    pallas_call x1, Pallas kernels, encode(): pl.pallas_call(functools.partial(enc_kernel, sp), out_shape=(jax.ShapeDty...  66.6 us

profile of v3, /device:TPU:0, one launch (start us, length us, event | category | flops | bytes accessed | tf_op | source)
XLA Modules:
  0.0 151.9 jit_solution(18438669029060648054)
XLA Ops:
  0.0 0.0 copy-start
  0.0 0.0 copy-start.3
  0.0 66.6 %encode.1 = (bf16[2,256,512]{2,1,0:T(8,128)(2,1)}, s32[8,2,256]{2,1,0:T(2,128)}, bf16[8,256,512]{2,1,0:T(8,128)(2,1)}) custom-call(s32[2,256]{1,0:T(2,128)} %mask_ref.1, bf16[2,256,1536]{2,1,0:T(8,128)(2,1)} %patches_h.1, bf16[256,1280]{1,0:T(8,128)(2,1)} %enc_pos_h.1, bf16[256,512]{1,0:T(8,128)(2,1)} %dec_pos_h.1, bf16[1536,1280]{1,0:T(8,128)(2,1)} %w_pe_h.1, ...), custom_call_target="tpu_custom_call" | custom-call | tf_op jit(solution)/shard_map/encode/pallas_call | solution.py:331
  66.7 0.0 copy-done.3
  66.7 0.0 copy-start.1
  66.7 1.0 copy-done.1
  67.7 0.0 copy-start.2
  67.7 0.7 copy-done.2
  68.4 80.8 %decode.1 = bf16[2,256,512]{2,1,0:T(8,128)(2,1)S(1)} custom-call(bf16[2,256,512]{2,1,0:T(8,128)(2,1)S(1)} %copy-done.1, s32[8,2,256]{2,1,0:T(2,128)S(1)} %copy-done.2, bf16[8,256,512]{2,1,0:T(8,128)(2,1)} %get-tuple-element.10.pos_h, bf16[512]{0:T(512)(128)(2,1)S(1)} %copy-done.3, bf16[2,1536,512]{2,1,0:T(8,128)(2,1)} %bitcast.14, ...), custom_call_target="tpu_custom_call" | custom-call | tf_op jit(solution)/shard_map/decode/pallas_call | solution.py:489
  149.2 0.0 copy-done
  149.2 2.7 %fusion = f32[2,256,1536]{2,1,0:T(8,128)} fusion(bf16[2,256,512]{2,1,0:T(8,128)(2,1)S(1)} %decode.1, bf16[512,1536]{1,0:T(8,128)(2,1)S(1)} %copy-done), kind=kOutput, calls=%fused_computation | convolution fusion | flops 805306368 | bytes 5242880 | tf_op jit(solution)/shard_map/cne,ep->cnp/dot_general | solution.py:520
Async XLA Ops:
  0.0 149.2 %copy-start = (bf16[512,1536]{1,0:T(8,128)(2,1)S(1)}, bf16[512,1536]{1,0:T(8,128)(2,1)}, u32[]{:S(2)}) copy-start(bf16[512,1536]{1,0:T(8,128)(2,1)} %param.33) | copy-start | bytes 4718596
  0.0 66.7 %copy-start.3 = (bf16[512]{0:T(512)(128)(2,1)S(1)}, bf16[512]{0:T(512)(128)(2,1)}, u32[]{:S(2)}) copy-start(bf16[512]{0:T(512)(128)(2,1)} %tok_ref.1) | copy-start | bytes 3076
  66.7 1.0 copy-start.1
  67.7 0.7 copy-start.2

commit v4 on v3

--- a/solution.py
+++ b/solution.py
@@ -87,13 +87,12 @@
 
 def enc_kernel(sp, mask_ref, patches_h, enc_pos_h, dec_pos_h, w_pe_h, b_pe_ref, qkv_h, proj_h, up_h, down_h, w_ed_h,
                z_all, mask_all, pos_all,
-               patches, enc_pos, w_pe, w_ed, wbuf, e_src, win, edge, hid, a_all, qkv_s, s_s, p_s, o_s, g_s, acc_s,
+               patches, enc_pos, w_pe, w_ed, wqkv, wproj, wup, wdown, x_s, e_src, tail_s, win, hid, a_all, qkv_s, s_s, p_s, o_s, g_s,
                wsem, insem, ms, mr, ws, wr, es, er, asend, arecv, zs, zr, pfs, pfr, pns, pnr, lsem):
     me = lax.axis_index('sp')
     n_clips, rows, width = patches.shape[0], patches.shape[1], hid.shape[1]
-    cap = e_src.shape[1]
-    share = cap // 2
-    half = share // 2
+    cap = e_src.shape[0] // n_clips
+    half = tail_s.shape[0] // n_clips
     n_layers = qkv_h.shape[0]
     my_rows = hid.shape[0]
     per = sp // n_clips
@@ -105,28 +104,83 @@
     my_half = me // per
     slot = lax.rem(me, per)
 
-    def chunk(l, j):
-        if j < 3:
-            src = qkv_h.at[l, pl.ds(j * width, width), :]
-        elif j == 3:
-            src = proj_h.at[l]
-        elif j < 8:
-            src = up_h.at[l, :, pl.ds((j - 4) * width, width)]
-        else:
-            src = down_h.at[l, pl.ds((j - 8) * width, width), :]
-        return pltpu.make_async_copy(src, wbuf.at[j], wsem.at[j])
+    def weight(l, i):
+        src, dst = ((qkv_h, wqkv), (proj_h, wproj), (up_h, wup), (down_h, wdown))[i]
+        return pltpu.make_async_copy(src.at[l], dst, wsem.at[i])
 
     loads = [pltpu.make_async_copy(a, b, insem.at[i]) for i, (a, b) in enumerate(
-        [(patches_h, patches), (w_pe_h, w_pe), (enc_pos_h, enc_pos), (w_ed_h, w_ed)])]
+        [(patches_h, patches), (enc_pos_h, enc_pos), (w_pe_h, w_pe), (w_ed_h, w_ed)])]
     for ld in loads:
         ld.start()
-    for j in range(12):
-        chunk(0, j).start()
 
     barrier = pltpu.get_barrier_semaphore()
     for k in range(1, sp):
         pl.semaphore_signal(barrier, inc=1, device_id={'sp': lax.rem(me + k, sp)}, device_id_type=MESH)
+
+    mask = mask_ref[...]
+    maskf = mask.astype(F32)
+    before = (lax.broadcasted_iota(jnp.int32, (rows, rows), 0) < lax.broadcasted_iota(jnp.int32, (rows, rows), 1))
+    mask8 = jnp.concatenate([maskf] + [jnp.zeros_like(maskf)] * 7, axis=0).astype(BF)
+    rank = mm(mask8, before.astype(BF)).astype(jnp.int32)
+    row_id = lax.broadcasted_iota(jnp.int32, (cap, rows), 0)
+    picks = []
+    for c in range(n_clips):
+        picks.append(jnp.where((row_id == rank[c:c + 1, :]) & (mask[c:c + 1, :] == 1), 1.0, 0.0))
+    pick2 = jnp.concatenate(picks, axis=0)
+    used = jnp.sum(pick2, axis=1, keepdims=True)
+    pick2 = pick2.astype(BF)
+    for ld in loads[:2]:
+        ld.wait()
+    for c in range(n_clips):
+        x_s[c * cap:(c + 1) * cap, :] = mm(pick2[c * cap:(c + 1) * cap], patches[c]).astype(BF)
+    fixed = used * b_pe_ref[...].reshape(1, width).astype(F32) + mm(pick2, enc_pos[...])
+    loads[2].wait()
+    for i in range(4):
+        weight(0, i).start()
+    e_src[...] = (mm(x_s[...], w_pe[...]) + fixed).astype(BF)
+    late = lax.broadcasted_iota(jnp.int32, (half, cap), 1) - lax.broadcasted_iota(jnp.int32, (half, cap), 0) + half
+    for c in range(n_clips):
+        count = jnp.sum(maskf[c:c + 1, :], axis=1, keepdims=True).astype(jnp.int32)
+        pick = jnp.where(late == count, 1.0, 0.0).astype(BF)
+        tail_s[c * half:(c + 1) * half, :] = mm(pick, e_src[c * cap:(c + 1) * cap, :]).astype(BF)
+
     pl.semaphore_wait(barrier, sp - 1)
+
+    def to(c, x, h):
+        return per * c + 2 * x + h
+
+    def send(c, x):
+        return pltpu.make_async_remote_copy(
+            src_ref=e_src.at[pl.ds(c * cap, cap)], dst_ref=win.at[pl.ds(pl.multiple_of(slot * cap, cap), cap)],
+            send_sem=ws.at[c, x], recv_sem=wr.at[slot], device_id={'sp': to(c, x, my_half)}, device_id_type=MESH)
+
+    last = per * cap
+    edges = ((per, 0, e_src, cap), (per - 1, 1, tail_s, half))
+
+    def send_edge(c, x, h, buf, step):
+        return pltpu.make_async_remote_copy(
+            src_ref=buf.at[pl.ds(c * step, half)], dst_ref=win.at[pl.ds(last, half)], send_sem=es.at[c, x], recv_sem=er,
+            device_id={'sp': to(c, x, h)}, device_id_type=MESH)
+
+    for c in range(n_clips):
+        for x in range(per // 2):
+            @pl.when(to(c, x, my_half) != me)
+            def _():
+                send(c, x).start()
+
+            @pl.when(to(c, x, my_half) == me)
+            def _():
+                pltpu.make_async_copy(
+                    e_src.at[pl.ds(c * cap, cap)], win.at[pl.ds(pl.multiple_of(slot * cap, cap), cap)], wr.at[slot]).start()
+
+            for src_dev, h, buf, step in edges:
+                @pl.when((me == src_dev) & (to(c, x, h) != me))
+                def _():
+                    send_edge(c, x, h, buf, step).start()
+
+                @pl.when((me == src_dev) & (to(c, x, h) == me))
+                def _():
+                    pltpu.make_async_copy(buf.at[pl.ds(c * step, half)], win.at[pl.ds(last, half)], er).start()
 
     mask_sends = []
     for k in range(1, sp):
@@ -136,118 +190,67 @@
         mask_sends[-1].start()
     own_mask = pltpu.make_async_copy(mask_ref, mask_all.at[me], lsem.at[0])
     own_mask.start()
-
-    mask = mask_ref[...]
-    maskf = mask.astype(F32)
-    before = (lax.broadcasted_iota(jnp.int32, (rows, rows), 0) < lax.broadcasted_iota(jnp.int32, (rows, rows), 1))
-    mask8 = jnp.concatenate([maskf] + [jnp.zeros_like(maskf)] * 7, axis=0).astype(BF)
-    rank = mm(mask8, before.astype(BF)).astype(jnp.int32)
-    b_row = b_pe_ref[...].reshape(1, width).astype(F32)
-    row_id = lax.broadcasted_iota(jnp.int32, (cap, rows), 0)
-    for ld in loads[:3]:
-        ld.wait()
-    local = []
-    for c in range(n_clips):
-        pick = (row_id == rank[c:c + 1, :]) & (mask[c:c + 1, :] == 1)
-        pick = jnp.where(pick, 1.0, 0.0)
-        used = jnp.sum(pick, axis=1, keepdims=True)
-        pick = pick.astype(BF)
-        x = mm(pick, patches[c]).astype(BF)
-        pos = mm(pick, enc_pos[...])
-        local.append((mm(x, w_pe[...]) + used * b_row + pos).astype(BF))
-
-    for ms_ in mask_sends:
-        ms_.wait_recv()
+    for m in mask_sends:
+        m.wait_recv()
     own_mask.wait()
-    total_before = [jnp.zeros((1, rows), F32) for _ in range(n_clips)]
+    starts = [jnp.zeros((1, 1), F32)]
     for s in range(sp):
-        ahead = jnp.where(s < me, 1.0, 0.0)
-        ms_row = mask_all[s].astype(F32)
-        for c in range(n_clips):
-            total_before[c] = total_before[c] + ahead * ms_row[c:c + 1, :]
-    sq0 = lax.broadcasted_iota(jnp.int32, (cap, cap), 0)
-    sq1 = lax.broadcasted_iota(jnp.int32, (cap, cap), 1)
-    for c in range(n_clips):
-        off = jnp.sum(total_before[c], axis=1, keepdims=True).astype(jnp.int32) - me * share + half
-        shift = jnp.where(sq0 == sq1 + off, 1.0, 0.0).astype(BF)
-        e_src[c] = mm(shift, local[c]).astype(BF)
-
-    def to(c, x, h):
-        return per * c + 2 * x + h
-
-    for c in range(n_clips):
-        for x in range(per // 2):
-            dst = to(c, x, my_half)
-
-            @pl.when(dst != me)
-            def _():
-                pltpu.make_async_remote_copy(
-                    src_ref=e_src.at[c], dst_ref=win.at[slot], send_sem=ws.at[c, x], recv_sem=wr.at[slot],
-                    device_id={'sp': dst}, device_id_type=MESH).start()
-
-            @pl.when(dst == me)
-            def _():
-                pltpu.make_async_copy(e_src.at[c], win.at[slot], wr.at[slot]).start()
-
-            for src_dev, h, r0 in ((per, 0, 0), (per - 1, 1, cap - half)):
-                edst = to(c, x, h)
-
-                @pl.when((me == src_dev) & (edst != me))
-                def _():
-                    pltpu.make_async_remote_copy(
-                        src_ref=e_src.at[c, pl.ds(r0, half)], dst_ref=edge, send_sem=es.at[c, x], recv_sem=er,
-                        device_id={'sp': edst}, device_id_type=MESH).start()
-
-                @pl.when((me == src_dev) & (edst == me))
-                def _():
-                    pltpu.make_async_copy(e_src.at[c, pl.ds(r0, half)], edge, er).start()
-
+        both = mask_all[s].astype(F32)
+        row = jnp.where(clip == 0, both[0:1, :], both[1:2, :])
+        starts.append(starts[-1] + jnp.sum(row, axis=1, keepdims=True))
+    out_row = lax.broadcasted_iota(jnp.int32, (my_rows, cap), 0) - lax.broadcasted_iota(jnp.int32, (my_rows, cap), 1)
+    places = []
     for b in range(per):
-        pltpu.make_async_copy(e_src.at[0], win.at[b], wr.at[b]).wait()
-    pltpu.make_async_copy(e_src.at[0, pl.ds(0, half)], edge, er).wait()
-
+        off = jnp.where(hf == 0, starts[b], starts[per + b] - my_rows).astype(jnp.int32)
+        places.append(jnp.where(out_row == off, 1.0, 0.0))
+    off = jnp.where(hf == 0, starts[per], starts[per] - half - my_rows).astype(jnp.int32)
+    places.append(jnp.where(out_row[:, :half] == off, 1.0, 0.0))
+    place_a = jnp.concatenate(places[:per], axis=1).astype(BF)
+    place_b = places[per].astype(BF)
+
+    for b in range(per):
+        pltpu.make_async_copy(e_src.at[pl.ds(0, cap)], win.at[pl.ds(b * cap, cap)], wr.at[b]).wait()
+    pltpu.make_async_copy(e_src.at[pl.ds(0, half)], win.at[pl.ds(last, half)], er).wait()
+    hid[...] = (mm(place_a, win[:last, :]) + mm(place_b, win[last:, :])).astype(BF)
+
+    scale = hd ** -0.5
     pos_own = pltpu.make_async_copy(dec_pos_h, pos_all.at[me], lsem.at[1])
     pos_own.start()
-    pos_far = []
-    for k in range(1, sp // 2):
-        pos_far.append(pltpu.make_async_remote_copy(
+
+    def pos_far(k):
+        return pltpu.make_async_remote_copy(
             src_ref=dec_pos_h, dst_ref=pos_all.at[me], send_sem=pfs.at[k], recv_sem=pfr.at[k],
-            device_id={'sp': lax.rem(me + 2 * k, sp)}, device_id_type=MESH))
-        pos_far[-1].start()
-
-    zero_edge = jnp.zeros((half, width), F32)
-    edge_v = edge[...].astype(F32)
-    first_prev = jnp.where(hf == 1, edge_v, zero_edge)
-    last_next = jnp.where(hf == 0, edge_v, zero_edge)
-    for b in range(per):
-        prev = first_prev if b == 0 else win[b - 1, cap - half:, :].astype(F32)
-        nxt = last_next if b == per - 1 else win[b + 1, :half, :].astype(F32)
-        lo = win[b, half:2 * half, :].astype(F32) + prev
-        hi = win[b, 2 * half:3 * half, :].astype(F32) + nxt
-        hid[b * share:b * share + half, :] = lo.astype(BF)
-        hid[b * share + half:(b + 1) * share, :] = hi.astype(BF)
-
-    scale = hd ** -0.5
+            device_id={'sp': lax.rem(me + 2 * k, sp)}, device_id_type=MESH)
+
+    def pos_near(k):
+        piece = lax.rem(me + 2 * k, sp)
+        return pltpu.make_async_remote_copy(
+            src_ref=pos_all.at[piece], dst_ref=pos_all.at[piece], send_sem=pns.at[k], recv_sem=pnr.at[k],
+            device_id={'sp': partner}, device_id_type=MESH)
 
     def layer(l, carry):
-        def refill(j):
+        def refill(i):
             @pl.when(l < n_layers - 1)
             def _():
-                chunk(l + 1, j).start()
+                weight(l + 1, i).start()
 
         a_all[l, 0] = norm_rows(hid[...])
         swap = pltpu.make_async_remote_copy(
             src_ref=a_all.at[l, 0], dst_ref=a_all.at[l, 1], send_sem=asend.at[l], recv_sem=arecv.at[l],
             device_id={'sp': partner}, device_id_type=MESH)
         swap.start()
+        weight(l, 0).wait()
         swap.wait()
-        rhs = a_all[l].reshape(2 * my_rows, width)
-        for j in range(3):
-            chunk(l, j).wait()
-            qkv_s[j] = mm(wbuf[j], rhs, NT).astype(BF)
-            refill(j)
+        qkv_s[...] = mm(wqkv[...], a_all[l].reshape(2 * my_rows, width), NT).astype(BF)
+        refill(0)
+
+        @pl.when(l == 0)
+        def _():
+            for k in range(1, sp // 2):
+                pos_far(k).start()
+
         for h in range(heads):
-            s_s[h] = mm(qkv_s[0, h * hd:(h + 1) * hd, :my_rows], qkv_s[1, h * hd:(h + 1) * hd, :], TN)
+            s_s[h] = mm(qkv_s[h * hd:(h + 1) * hd, :my_rows], qkv_s[width + h * hd:width + (h + 1) * hd, :], TN)
 
         def soft(i, cc):
             s = s_s[i] * scale
@@ -257,67 +260,68 @@
 
         lax.fori_loop(0, heads, soft, 0, unroll=4)
         for h in range(heads):
-            o_s[h * hd:(h + 1) * hd, :] = mm(qkv_s[2, h * hd:(h + 1) * hd, :], p_s[h], NT).astype(BF)
-        chunk(l, 3).wait()
-        h1 = (hid[...].astype(F32) + mm(o_s[...], wbuf[3], TN)).astype(BF)
+            o_s[h * hd:(h + 1) * hd, :] = mm(qkv_s[2 * width + h * hd:2 * width + (h + 1) * hd, :], p_s[h], NT).astype(BF)
+        weight(l, 1).wait()
+        h1 = (hid[...].astype(F32) + mm(o_s[...], wproj[...], TN)).astype(BF)
         hid[...] = h1
+        refill(1)
+        a2 = norm_rows(h1)
+        weight(l, 2).wait()
+        g_s[...] = gelu(mm(a2, wup[...])).astype(BF)
+        refill(2)
+
+        @pl.when(l == n_layers - 1)
+        def _():
+            pos_own.wait()
+            for k in range(1, sp // 2):
+                pos_far(k).wait_recv()
+            for k in range(sp // 2):
+                pos_near(k).start()
+
+        weight(l, 3).wait()
+        hid[...] = (hid[...].astype(F32) + mm(g_s[...], wdown[...])).astype(BF)
         refill(3)
-        a2 = norm_rows(h1)
-        for j in range(4):
-            chunk(l, 4 + j).wait()
-            g_s[:, j * width:(j + 1) * width] = gelu(mm(a2, wbuf[4 + j])).astype(BF)
-            refill(4 + j)
-        for j in range(4):
-            chunk(l, 8 + j).wait()
-            part = mm(g_s[:, j * width:(j + 1) * width], wbuf[8 + j])
-            acc_s[...] = part if j == 0 else acc_s[...] + part
-            refill(8 + j)
-        hid[...] = (hid[...].astype(F32) + acc_s[...]).astype(BF)
         return carry
 
     lax.fori_loop(0, n_layers, layer, 0)
 
-    for p in pos_far:
-        p.wait()
-    pos_own.wait()
-    pos_near = []
-    for k in range(sp // 2):
-        piece = lax.rem(me + 2 * k, sp)
-        pos_near.append(pltpu.make_async_remote_copy(
-            src_ref=pos_all.at[piece], dst_ref=pos_all.at[piece], send_sem=pns.at[k], recv_sem=pnr.at[k],
-            device_id={'sp': partner}, device_id_type=MESH))
-        pos_near[-1].start()
-
     loads[3].wait()
-    mine = z_all.at[clip, pl.ds(pl.multiple_of(hf * my_rows, my_rows), my_rows), :]
-    z_all[clip, pl.ds(pl.multiple_of(hf * my_rows, my_rows), my_rows), :] = mm(norm_rows(hid[...]), w_ed[...]).astype(BF)
-    z_sends = []
-    across = lax.rem(me + per, sp)
-    for i, dst in enumerate((across, across + 1 - 2 * hf, partner)):
-        z_sends.append(pltpu.make_async_remote_copy(
-            src_ref=mine, dst_ref=mine, send_sem=zs.at[i], recv_sem=zr.at[i],
-            device_id={'sp': dst}, device_id_type=MESH))
-        z_sends[-1].start()
-    for k in mask_sends:
-        k.wait_send()
+    at = pl.multiple_of(hf * my_rows, my_rows)
+    mine = z_all.at[clip, pl.ds(at, my_rows), :]
+    other_clip = n_clips - 1 - clip
+    theirs = z_all.at[other_clip, pl.ds(at, my_rows), :]
+    z_all[clip, pl.ds(at, my_rows), :] = mm(norm_rows(hid[...]), w_ed[...]).astype(BF)
+
+    def z_send(i, ref, dst):
+        return pltpu.make_async_remote_copy(
+            src_ref=ref, dst_ref=ref, send_sem=zs.at[i], recv_sem=zr.at[i], device_id={'sp': dst}, device_id_type=MESH)
+
+    across = z_send(0, mine, lax.rem(me + per, sp))
+    beside = z_send(1, mine, partner)
+    relay = z_send(2, theirs, partner)
+    across.start()
+    beside.start()
+    for m in mask_sends:
+        m.wait_send()
     for c in range(n_clips):
         for x in range(per // 2):
             @pl.when(to(c, x, my_half) != me)
             def _():
-                pltpu.make_async_remote_copy(
-                    src_ref=e_src.at[c], dst_ref=win.at[slot], send_sem=ws.at[c, x], recv_sem=wr.at[slot],
-                    device_id={'sp': to(c, x, my_half)}, device_id_type=MESH).wait_send()
-
-            for src_dev, h, r0 in ((per, 0, 0), (per - 1, 1, cap - half)):
+                send(c, x).wait_send()
+
+            for src_dev, h, buf, step in edges:
                 @pl.when((me == src_dev) & (to(c, x, h) != me))
                 def _():
-                    pltpu.make_async_remote_copy(
-                        src_ref=e_src.at[c, pl.ds(r0, half)], dst_ref=edge, send_sem=es.at[c, x], recv_sem=er,
-                        device_id={'sp': to(c, x, h)}, device_id_type=MESH).wait_send()
-    for p in pos_near:
-        p.wait()
-    for s in z_sends:
-        s.wait()
+                    send_edge(c, x, h, buf, step).wait_send()
+    for k in range(1, sp // 2):
+        pos_far(k).wait_send()
+    across.wait_recv()
+    relay.start()
+    for k in range(sp // 2):
+        pos_near(k).wait()
+    across.wait_send()
+    beside.wait()
+    relay.wait()
 
 
 def encode(sp, vis_mask, patches, enc_pos, dec_pos, w_pe, b_pe, qkv_t, proj, up, down, w_ed):
@@ -325,9 +329,11 @@
     width = w_pe.shape[1]
     d_width = w_ed.shape[1]
     cap = 2 * rows // KEEP_DIV
+    half = cap // 4
     my_rows = rows * sp // KEEP_DIV // 2
     dma = pltpu.SemaphoreType.DMA
     per = sp // n_clips
+    far = sp // 2
     return pl.pallas_call(
         functools.partial(enc_kernel, sp),
         out_shape=(jax.ShapeDtypeStruct((n_clips, 2 * my_rows, d_width), BF),
@@ -337,16 +343,17 @@
         out_specs=(VMEM, VMEM, ANY),
         scratch_shapes=[
             pltpu.VMEM(patches.shape, BF), pltpu.VMEM(enc_pos.shape, BF), pltpu.VMEM(w_pe.shape, BF), pltpu.VMEM(w_ed.shape, BF),
-            pltpu.VMEM((12, width, width), BF),
-            pltpu.VMEM((n_clips, cap, width), BF), pltpu.VMEM((per, cap, width), BF), pltpu.VMEM((cap // 4, width), BF),
+            pltpu.VMEM(qkv_t.shape[1:], BF), pltpu.VMEM(proj.shape[1:], BF), pltpu.VMEM(up.shape[1:], BF), pltpu.VMEM(down.shape[1:], BF),
+            pltpu.VMEM((n_clips * cap, p_width), BF), pltpu.VMEM((n_clips * cap, width), BF), pltpu.VMEM((n_clips * half, width), BF),
+            pltpu.VMEM((per * cap + half, width), BF),
             pltpu.VMEM((my_rows, width), BF), pltpu.VMEM((qkv_t.shape[0], 2, my_rows, width), BF),
-            pltpu.VMEM((3, width, 2 * my_rows), BF),
+            pltpu.VMEM((3 * width, 2 * my_rows), BF),
             pltpu.VMEM((16, my_rows, 2 * my_rows), F32), pltpu.VMEM((16, my_rows, 2 * my_rows), BF),
-            pltpu.VMEM((width, my_rows), BF), pltpu.VMEM((my_rows, 4 * width), BF), pltpu.VMEM((my_rows, width), F32),
-            dma((12,)), dma((4,)), dma((sp,)), dma((sp,)), dma((n_clips, per // 2)), dma((per,)), dma((n_clips, per // 2)), dma,
-            dma((2,)), dma((2,)), dma((3,)), dma((3,)), dma((sp // 2,)), dma((sp // 2,)), dma((sp // 2,)), dma((sp // 2,)), dma((2,)),
+            pltpu.VMEM((width, my_rows), BF), pltpu.VMEM((my_rows, 4 * width), BF),
+            dma((4,)), dma((4,)), dma((sp,)), dma((sp,)), dma((n_clips, per // 2)), dma((per,)), dma((n_clips, per // 2)), dma,
+            dma((2,)), dma((2,)), dma((3,)), dma((3,)), dma((far,)), dma((far,)), dma((far,)), dma((far,)), dma((2,)),
         ],
-        compiler_params=pltpu.CompilerParams(collective_id=1, has_side_effects=True, vmem_limit_bytes=62 << 20),
+        compiler_params=pltpu.CompilerParams(collective_id=1, has_side_effects=True, vmem_limit_bytes=63 << 20),
         name='encode',
     )(vis_mask, patches, enc_pos, dec_pos, w_pe, b_pe, qkv_t, proj, up, down, w_ed)
 
@@ -382,7 +389,7 @@
             vis = m[s:s + 1, :]
             rank_s[c, s:s + 1, :] = jnp.where(vis == 1, (local[s:s + 1, :] + base).astype(jnp.int32), n_vis)
             base = base + jnp.sum(vis.astype(F32), axis=1, keepdims=True)
-    for ld in loads:
+    for ld in loads[:2]:
         ld.wait()
 
     def far(c, k):
@@ -433,6 +440,11 @@
 
         lax.fori_loop(0, sp, block, 0)
         attend(0, c)
+
+        @pl.when(c == 0)
+        def _():
+            for ld in loads[2:]:
+                ld.wait()
 
         @pl.when(c == 1)
         def _():

time: 152 us -> 140 us (0.921)
  Pallas kernels: 147 us -> 135 us
    pallas_call x1, Pallas kernels: 66.6 us -> 57 us  [encode(): pl.pallas_call(functools.partial(enc_kernel, sp), out_shape=(jax.ShapeDty...]
    pallas_call x1, Pallas kernels: 80.8 us -> 78.2 us  [decode(): pl.pallas_call(functools.partial(decode_kernel, sp), out_shape=jax.ShapeD...]
where the time goes in v4:
time: 140 us
  Pallas kernels  135 us (96%)
  matrix products  2.65 us (2%)
  local copies, waits for them, and re-layouts  1.76 us (1%)
    pallas_call x1, Pallas kernels, decode(): pl.pallas_call(functools.partial(decode_kernel, sp), out_shape=jax.ShapeD...  78.2 us
    pallas_call x1, Pallas kernels, encode(): pl.pallas_call(functools.partial(enc_kernel, sp), out_shape=(jax.ShapeDty...  57 us

profile of v4, /device:TPU:0, one launch (start us, length us, event | category | flops | bytes accessed | tf_op | source)
XLA Modules:
  0.0 139.6 jit_solution(11356919772137784687)
XLA Ops:
  0.0 0.0 copy-start.2
  0.0 57.0 %encode.1 = (bf16[2,256,512]{2,1,0:T(8,128)(2,1)}, s32[8,2,256]{2,1,0:T(2,128)}, bf16[8,256,512]{2,1,0:T(8,128)(2,1)}) custom-call(s32[2,256]{1,0:T(2,128)} %mask_ref.1, bf16[2,256,1536]{2,1,0:T(8,128)(2,1)} %patches_h.1, bf16[256,1280]{1,0:T(8,128)(2,1)} %enc_pos_h.1, bf16[256,512]{1,0:T(8,128)(2,1)} %dec_pos_h.1, bf16[1536,1280]{1,0:T(8,128)(2,1)} %w_pe_h.1, ...), custom_call_target="tpu_custom_call" | custom-call | tf_op jit(solution)/shard_map/encode/pallas_call | solution.py:337
  57.0 0.0 copy-done.2
  57.0 0.0 copy-start
  57.0 1.0 copy-done
  58.1 0.0 copy-start.1
  58.1 0.7 copy-done.1
  58.8 0.0 copy-start.3
  58.8 78.2 %decode.1 = bf16[2,256,512]{2,1,0:T(8,128)(2,1)S(1)} custom-call(bf16[2,256,512]{2,1,0:T(8,128)(2,1)S(1)} %copy-done, s32[8,2,256]{2,1,0:T(2,128)S(1)} %copy-done.1, bf16[8,256,512]{2,1,0:T(8,128)(2,1)} %get-tuple-element.10.pos_h, bf16[512]{0:T(512)(128)(2,1)S(1)} %copy-done.2, bf16[2,1536,512]{2,1,0:T(8,128)(2,1)} %bitcast.14, ...), custom_call_target="tpu_custom_call" | custom-call | tf_op jit(solution)/shard_map/decode/pallas_call | solution.py:501
  137.0 0.0 copy-done.3
  137.0 2.6 %fusion = f32[2,256,1536]{2,1,0:T(8,128)} fusion(bf16[2,256,512]{2,1,0:T(8,128)(2,1)S(1)} %decode.1, bf16[512,1536]{1,0:T(8,128)(2,1)S(1)} %copy-done.3), kind=kOutput, calls=%fused_computation | convolution fusion | flops 805306368 | bytes 5242880 | tf_op jit(solution)/shard_map/cne,ep->cnp/dot_general | solution.py:532
Async XLA Ops:
  0.0 57.0 %copy-start.2 = (bf16[512]{0:T(512)(128)(2,1)S(1)}, bf16[512]{0:T(512)(128)(2,1)}, u32[]{:S(2)}) copy-start(bf16[512]{0:T(512)(128)(2,1)} %tok_ref.1) | copy-start | bytes 3076
  57.0 1.0 copy-start
  58.1 0.7 copy-start.1
  58.8 78.2 %copy-start.3 = (bf16[512,1536]{1,0:T(8,128)(2,1)S(1)}, bf16[512,1536]{1,0:T(8,128)(2,1)}, u32[]{:S(2)}) copy-start(bf16[512,1536]{1,0:T(8,128)(2,1)} %param.33) | copy-start | bytes 4718596

commit v5 on v4

--- a/solution.py
+++ b/solution.py
@@ -85,10 +85,10 @@
     lax.fori_loop(0, heads // 2, body, first)
 
 
-def enc_kernel(sp, mask_ref, patches_h, enc_pos_h, dec_pos_h, w_pe_h, b_pe_ref, qkv_h, proj_h, up_h, down_h, w_ed_h,
-               z_all, mask_all, pos_all,
-               patches, enc_pos, w_pe, w_ed, wqkv, wproj, wup, wdown, x_s, e_src, tail_s, win, hid, a_all, qkv_s, s_s, p_s, o_s, g_s,
-               wsem, insem, ms, mr, ws, wr, es, er, asend, arecv, zs, zr, pfs, pfr, pns, pnr, lsem):
+def enc_kernel(sp, mask_ref, patches_h, enc_pos_h, dec_pos_h, w_pe_h, b_pe_ref, qkv_h, proj_h, up_h, down_h,
+               hid_out, mask_all, pos_all,
+               patches, enc_pos, w_pe, wqkv, wproj, wup, wdown, x_s, e_src, tail_s, win, hid, a_all, qkv_s, s_s, p_s, o_s, g_s,
+               wsem, insem, ms, mr, ws, wr, es, er, asend, arecv, pfs, pfr, pns, pnr, lsem):
     me = lax.axis_index('sp')
     n_clips, rows, width = patches.shape[0], patches.shape[1], hid.shape[1]
     cap = e_src.shape[0] // n_clips
@@ -109,7 +109,7 @@
         return pltpu.make_async_copy(src.at[l], dst, wsem.at[i])
 
     loads = [pltpu.make_async_copy(a, b, insem.at[i]) for i, (a, b) in enumerate(
-        [(patches_h, patches), (enc_pos_h, enc_pos), (w_pe_h, w_pe), (w_ed_h, w_ed)])]
+        [(patches_h, patches), (enc_pos_h, enc_pos), (w_pe_h, w_pe)])]
     for ld in loads:
         ld.start()
 
@@ -240,8 +240,9 @@
             device_id={'sp': partner}, device_id_type=MESH)
         swap.start()
         weight(l, 0).wait()
+        qkv_s[:width, :my_rows] = mm(wqkv[:width, :], a_all[l, 0], NT).astype(BF)
         swap.wait()
-        qkv_s[...] = mm(wqkv[...], a_all[l].reshape(2 * my_rows, width), NT).astype(BF)
+        qkv_s[width:, :] = mm(wqkv[width:, :], a_all[l].reshape(2 * my_rows, width), NT).astype(BF)
         refill(0)
 
         @pl.when(l == 0)
@@ -285,22 +286,7 @@
 
     lax.fori_loop(0, n_layers, layer, 0)
 
-    loads[3].wait()
-    at = pl.multiple_of(hf * my_rows, my_rows)
-    mine = z_all.at[clip, pl.ds(at, my_rows), :]
-    other_clip = n_clips - 1 - clip
-    theirs = z_all.at[other_clip, pl.ds(at, my_rows), :]
-    z_all[clip, pl.ds(at, my_rows), :] = mm(norm_rows(hid[...]), w_ed[...]).astype(BF)
-
-    def z_send(i, ref, dst):
-        return pltpu.make_async_remote_copy(
-            src_ref=ref, dst_ref=ref, send_sem=zs.at[i], recv_sem=zr.at[i], device_id={'sp': dst}, device_id_type=MESH)
-
-    across = z_send(0, mine, lax.rem(me + per, sp))
-    beside = z_send(1, mine, partner)
-    relay = z_send(2, theirs, partner)
-    across.start()
-    beside.start()
+    hid_out[...] = hid[...]
     for m in mask_sends:
         m.wait_send()
     for c in range(n_clips):
@@ -315,19 +301,14 @@
                     send_edge(c, x, h, buf, step).wait_send()
     for k in range(1, sp // 2):
         pos_far(k).wait_send()
-    across.wait_recv()
-    relay.start()
     for k in range(sp // 2):
         pos_near(k).wait()
-    across.wait_send()
-    beside.wait()
-    relay.wait()
-
-
-def encode(sp, vis_mask, patches, enc_pos, dec_pos, w_pe, b_pe, qkv_t, proj, up, down, w_ed):
+
+
+def encode(sp, vis_mask, patches, enc_pos, dec_pos, w_pe, b_pe, qkv_t, proj, up, down):
     n_clips, rows, p_width = patches.shape
     width = w_pe.shape[1]
-    d_width = w_ed.shape[1]
+    d_width = dec_pos.shape[1]
     cap = 2 * rows // KEEP_DIV
     half = cap // 4
     my_rows = rows * sp // KEEP_DIV // 2
@@ -336,13 +317,13 @@
     far = sp // 2
     return pl.pallas_call(
         functools.partial(enc_kernel, sp),
-        out_shape=(jax.ShapeDtypeStruct((n_clips, 2 * my_rows, d_width), BF),
+        out_shape=(jax.ShapeDtypeStruct((my_rows, width), BF),
                    jax.ShapeDtypeStruct((sp, n_clips, rows), jnp.int32),
                    jax.ShapeDtypeStruct((sp, rows, d_width), BF)),
-        in_specs=[VMEM, ANY, ANY, ANY, ANY, VMEM, ANY, ANY, ANY, ANY, ANY],
+        in_specs=[VMEM, ANY, ANY, ANY, ANY, VMEM, ANY, ANY, ANY, ANY],
         out_specs=(VMEM, VMEM, ANY),
         scratch_shapes=[
-            pltpu.VMEM(patches.shape, BF), pltpu.VMEM(enc_pos.shape, BF), pltpu.VMEM(w_pe.shape, BF), pltpu.VMEM(w_ed.shape, BF),
+            pltpu.VMEM(patches.shape, BF), pltpu.VMEM(enc_pos.shape, BF), pltpu.VMEM(w_pe.shape, BF),
             pltpu.VMEM(qkv_t.shape[1:], BF), pltpu.VMEM(proj.shape[1:], BF), pltpu.VMEM(up.shape[1:], BF), pltpu.VMEM(down.shape[1:], BF),
             pltpu.VMEM((n_clips * cap, p_width), BF), pltpu.VMEM((n_clips * cap, width), BF), pltpu.VMEM((n_clips * half, width), BF),
             pltpu.VMEM((per * cap + half, width), BF),
@@ -351,36 +332,57 @@
             pltpu.VMEM((16, my_rows, 2 * my_rows), F32), pltpu.VMEM((16, my_rows, 2 * my_rows), BF),
             pltpu.VMEM((width, my_rows), BF), pltpu.VMEM((my_rows, 4 * width), BF),
             dma((4,)), dma((4,)), dma((sp,)), dma((sp,)), dma((n_clips, per // 2)), dma((per,)), dma((n_clips, per // 2)), dma,
-            dma((2,)), dma((2,)), dma((3,)), dma((3,)), dma((far,)), dma((far,)), dma((far,)), dma((far,)), dma((2,)),
+            dma((2,)), dma((2,)), dma((far,)), dma((far,)), dma((far,)), dma((far,)), dma((2,)),
         ],
         compiler_params=pltpu.CompilerParams(collective_id=1, has_side_effects=True, vmem_limit_bytes=63 << 20),
         name='encode',
-    )(vis_mask, patches, enc_pos, dec_pos, w_pe, b_pe, qkv_t, proj, up, down, w_ed)
-
-
-def decode_kernel(sp, z_ref, mask_all, pos_h, tok_ref, wqkv_h, wproj_h, wup_h, wdown_h, a_out,
-                  pos, wqkv, wproj, wup, wdown, rank_s, u_s, a_own, a_all, k_s, vt_s, q_s, s_s, o_s,
-                  insem, fs, fr, ns, nr):
+    )(vis_mask, patches, enc_pos, dec_pos, w_pe, b_pe, qkv_t, proj, up, down)
+
+
+def decode_kernel(sp, hid_h, w_ed_h, mask_h, pos_h, tok_ref, wqkv_h, wproj_h, wup_h, wdown_h, a_out,
+                  hid, w_ed, mask_all, pos, wqkv, wproj, wup, wdown, z_s, rank_s, u_s, a_own, a_all, km_s, vm_s, pv_s, k_s, vt_s, q_s, s_s, o_s,
+                  insem, zs, zr, fs, fr, ns, nr):
     me = lax.axis_index('sp')
-    partner = me + 1 - 2 * lax.rem(me, 2)
-    n_clips, n_vis, width = z_ref.shape
+    hf = lax.rem(me, 2)
+    partner = me + 1 - 2 * hf
+    n_clips, n_vis, width = z_s.shape
     rows = mask_all.shape[2]
+    my_rows = hid.shape[0]
+    per = sp // n_clips
+    clip_of = me // per
     tok = rows * sp
     heads, hd = 16, width // 16
     n_far = sp // 2
 
     loads = [pltpu.make_async_copy(a, b, insem.at[i]) for i, (a, b) in enumerate(
-        [(pos_h, pos), (wqkv_h, wqkv), (wproj_h, wproj), (wup_h, wup), (wdown_h, wdown)])]
+        [(hid_h, hid), (w_ed_h, w_ed), (mask_h, mask_all), (pos_h, pos), (wqkv_h, wqkv), (wproj_h, wproj), (wup_h, wup), (wdown_h, wdown)])]
     for ld in loads:
         ld.start()
     barrier = pltpu.get_barrier_semaphore()
     for k in range(1, sp):
         pl.semaphore_signal(barrier, inc=1, device_id={'sp': lax.rem(me + k, sp)}, device_id_type=MESH)
+
+    at = pl.multiple_of(hf * my_rows, my_rows)
+    mine = z_s.at[clip_of, pl.ds(at, my_rows), :]
+    theirs = z_s.at[n_clips - 1 - clip_of, pl.ds(at, my_rows), :]
+    for ld in loads[:2]:
+        ld.wait()
+    z_s[clip_of, pl.ds(at, my_rows), :] = mm(norm_rows(hid[...]), w_ed[...]).astype(BF)
     pl.semaphore_wait(barrier, sp - 1)
 
+    def z_send(i, ref, dst):
+        return pltpu.make_async_remote_copy(
+            src_ref=ref, dst_ref=ref, send_sem=zs.at[i], recv_sem=zr.at[i], device_id={'sp': dst}, device_id_type=MESH)
+
+    across = z_send(0, mine, lax.rem(me + per, sp))
+    beside = z_send(1, mine, partner)
+    relayed = z_send(2, theirs, partner)
+    across.start()
+    beside.start()
+
     before = (lax.broadcasted_iota(jnp.int32, (rows, rows), 0) < lax.broadcasted_iota(jnp.int32, (rows, rows), 1)).astype(BF)
-    pad = 16
-    row_id = lax.broadcasted_iota(jnp.int32, (n_vis + pad, rows), 0)
+    row_id = lax.broadcasted_iota(jnp.int32, (n_vis, rows), 0)
+    loads[2].wait()
     for c in range(n_clips):
         m = mask_all[:, c, :]
         local = mm(m.astype(F32).astype(BF), before)
@@ -389,8 +391,27 @@
             vis = m[s:s + 1, :]
             rank_s[c, s:s + 1, :] = jnp.where(vis == 1, (local[s:s + 1, :] + base).astype(jnp.int32), n_vis)
             base = base + jnp.sum(vis.astype(F32), axis=1, keepdims=True)
-    for ld in loads[:2]:
+    for ld in loads[3:5]:
         ld.wait()
+
+    def pick_of(c, b):
+        return jnp.where(row_id == rank_s[c, pl.ds(b, 1), :], 1.0, 0.0).astype(BF)
+
+    def keys_values(l, b, blk, k_to, vt_to):
+        here = pl.ds(pl.multiple_of(b * rows, rows), rows)
+        k_to[here, :] = mm(blk, wqkv[l, width:2 * width, :], NT).astype(BF)
+        vt_to[:, here] = mm(wqkv[l, 2 * width:, :], blk, NT).astype(BF)
+
+    token = tok_ref[...].reshape(1, width).astype(F32)
+    pv_s[...] = jnp.zeros_like(pv_s)
+
+    def plain(b, cc):
+        keys_values(0, b, norm_rows((token + pos[b].astype(F32)).astype(BF)), km_s, vm_s)
+        for c in range(n_clips):
+            pv_s[c] += mm(pick_of(c, b), pos[b])
+        return cc
+
+    lax.fori_loop(0, sp, plain, 0)
 
     def far(c, k):
         return pltpu.make_async_remote_copy(
@@ -409,11 +430,6 @@
         for k in range(n_far):
             near(c, k).start()
 
-    def keys_values(l, b, blk):
-        at = pl.multiple_of(b * rows, rows)
-        k_s[pl.ds(at, rows), :] = mm(blk, wqkv[l, width:2 * width, :], NT).astype(BF)
-        vt_s[:, pl.ds(at, rows)] = mm(wqkv[l, 2 * width:, :], blk, NT).astype(BF)
-
     def attend(l, c):
         q_s[...] = mm(wqkv[l, :width, :], a_own[c], NT).astype(BF)
         attend_clip(tok, rows, heads, hd, k_s, vt_s, q_s, s_s, o_s)
@@ -423,27 +439,41 @@
         g = gelu(mm(norm_rows(h1), wup[l])).astype(BF)
         return (h1.astype(F32) + mm(g, wdown[l])).astype(BF)
 
+    across.wait_recv()
+    relayed.start()
+    beside.wait_recv()
+    relayed.wait_recv()
+
     def first(c, carry):
-        z_aug = jnp.concatenate([z_ref[c], tok_ref[...].reshape(1, width), jnp.zeros((pad - 1, width), BF)], axis=0)
+        u_vis = (z_s[c].astype(F32) + pv_s[c]).astype(BF)
+        a_vis = norm_rows(u_vis)
+        k_vis = mm(a_vis, wqkv[0, width:2 * width, :], NT).astype(BF)
+        vt_vis = mm(wqkv[0, 2 * width:, :], a_vis, NT).astype(BF)
+        k_aug = jnp.concatenate([k_vis, jnp.ones((n_vis, 128), BF)], axis=1)
+        u_aug = jnp.concatenate([u_vis, jnp.ones((n_vis, 128), BF)], axis=1)
+
+        def put(pick, aug, plain_rows):
+            got = mm(pick, aug, TN)
+            seen = jnp.concatenate([got[:, width:]] * (width // 128), axis=1)
+            return jnp.where(seen > 0.5, got[:, :width], plain_rows.astype(F32)).astype(BF)
 
         def block(b, cc):
-            pick = jnp.where(row_id == rank_s[c, pl.ds(b, 1), :], 1.0, 0.0).astype(BF)
-            u = (mm(pick, z_aug, TN) + pos[b].astype(F32)).astype(BF)
-            a = norm_rows(u)
-            keys_values(0, b, a)
-
-            @pl.when(b == me)
-            def _():
-                u_s[c] = u
-                a_own[c] = a
+            here = pl.ds(pl.multiple_of(b * rows, rows), rows)
+            pick = pick_of(c, b)
+            k_s[here, :] = put(pick, k_aug, km_s[here, :])
+            seen = rank_s[c, pl.ds(b, 1), :] < n_vis
+            vt_s[:, here] = jnp.where(seen, mm(vt_vis, pick), vm_s[:, here].astype(F32)).astype(BF)
             return cc
 
         lax.fori_loop(0, sp, block, 0)
+        u = put(pick_of(c, me), u_aug, (token + pos[me].astype(F32)).astype(BF))
+        u_s[c] = u
+        a_own[c] = norm_rows(u)
         attend(0, c)
 
         @pl.when(c == 0)
         def _():
-            for ld in loads[2:]:
+            for ld in loads[5:]:
                 ld.wait()
 
         @pl.when(c == 1)
@@ -460,16 +490,16 @@
     lax.fori_loop(0, n_clips, first, 0)
 
     def second(c, carry):
-        keys_values(1, me, a_own[c])
+        keys_values(1, me, a_own[c], k_s, vt_s)
 
         def same(k, cc):
             b = lax.rem(me + 2 * k, sp)
-            keys_values(1, b, a_all[c, b])
+            keys_values(1, b, a_all[c, b], k_s, vt_s)
             return cc
 
         def other(k, cc):
             b = lax.rem(partner + 2 * k, sp)
-            keys_values(1, b, a_all[c, b])
+            keys_values(1, b, a_all[c, b], k_s, vt_s)
             return cc
 
         lax.fori_loop(1, n_far, same, 0)
@@ -491,30 +521,37 @@
             near(c, k).wait_send()
             if k:
                 far(c, k).wait_send()
-
-
-def decode(sp, z_all, mask_all, pos_all, mask_token, wqkv, wproj, wup, wdown):
-    n_clips, n_vis, width = z_all.shape
-    rows = mask_all.shape[2]
+    across.wait_send()
+    beside.wait_send()
+    relayed.wait_send()
+
+
+def decode(sp, hid, w_ed, mask_all, pos_all, mask_token, wqkv, wproj, wup, wdown):
+    _, n_clips, rows = mask_all.shape
+    width = w_ed.shape[1]
     tok = rows * sp
+    n_vis = tok // KEEP_DIV
     dma = pltpu.SemaphoreType.DMA
     return pl.pallas_call(
         functools.partial(decode_kernel, sp),
         out_shape=jax.ShapeDtypeStruct((n_clips, rows, width), BF),
-        in_specs=[VMEM, VMEM, ANY, VMEM, ANY, ANY, ANY, ANY],
+        in_specs=[ANY, ANY, ANY, ANY, VMEM, ANY, ANY, ANY, ANY],
         out_specs=VMEM,
         scratch_shapes=[
+            pltpu.VMEM(hid.shape, BF), pltpu.VMEM(w_ed.shape, BF), pltpu.VMEM(mask_all.shape, jnp.int32),
             pltpu.VMEM(pos_all.shape, BF), pltpu.VMEM(wqkv.shape, BF), pltpu.VMEM(wproj.shape, BF),
             pltpu.VMEM(wup.shape, BF), pltpu.VMEM(wdown.shape, BF),
+            pltpu.VMEM((n_clips, n_vis, width), BF),
             pltpu.VMEM((n_clips, sp, rows), jnp.int32), pltpu.VMEM((n_clips, rows, width), BF), pltpu.VMEM((n_clips, rows, width), BF),
             pltpu.VMEM((n_clips, sp, rows, width), BF),
+            pltpu.VMEM((tok, width), BF), pltpu.VMEM((width, tok), BF), pltpu.VMEM((n_clips, n_vis, width), F32),
             pltpu.VMEM((tok, width), BF), pltpu.VMEM((width, tok), BF), pltpu.VMEM((width, rows), BF),
             pltpu.VMEM((2, tok, rows), F32), pltpu.VMEM((width, rows), BF),
-            dma((5,)), dma((n_clips, sp // 2)), dma((n_clips, sp // 2)), dma((n_clips, sp // 2)), dma((n_clips, sp // 2)),
+            dma((8,)), dma((3,)), dma((3,)), dma((n_clips, sp // 2)), dma((n_clips, sp // 2)), dma((n_clips, sp // 2)), dma((n_clips, sp // 2)),
         ],
-        compiler_params=pltpu.CompilerParams(collective_id=2, has_side_effects=True, vmem_limit_bytes=52 << 20),
+        compiler_params=pltpu.CompilerParams(collective_id=2, has_side_effects=True, vmem_limit_bytes=56 << 20),
         name='decode',
-    )(z_all, mask_all, pos_all, mask_token, wqkv, wproj, wup, wdown)
+    )(hid, w_ed, mask_all, pos_all, mask_token, wqkv, wproj, wup, wdown)
 
 
 def solution(mesh):
@@ -525,9 +562,9 @@
         d_width = dec_qkv.shape[1]
         enc_qkv_t = jnp.transpose(enc_qkv, (0, 2, 3, 4, 1)).reshape(n_layers, 3 * width, width)
         dec_qkv_t = jnp.transpose(dec_qkv, (0, 2, 3, 4, 1)).reshape(n_layers, 3 * d_width, d_width)
-        z_all, mask_all, pos_all = encode(sp, vis_mask, patches, enc_pos, dec_pos, w_pe, b_pe, enc_qkv_t,
-                                          enc_proj.reshape(n_layers, width, width), enc_up, enc_down, w_ed)
-        acts = decode(sp, z_all, mask_all, pos_all, mask_token, dec_qkv_t,
+        hid, mask_all, pos_all = encode(sp, vis_mask, patches, enc_pos, dec_pos, w_pe, b_pe, enc_qkv_t,
+                                          enc_proj.reshape(n_layers, width, width), enc_up, enc_down)
+        acts = decode(sp, hid, w_ed, mask_all, pos_all, mask_token, dec_qkv_t,
                       dec_proj.reshape(n_layers, d_width, d_width), dec_up, dec_down)
         return jnp.einsum('cne,ep->cnp', acts, w_out, preferred_element_type=F32)
 

time: 140 us -> 130 us (0.929)
  Pallas kernels: 135 us -> 126 us
  local copies, waits for them, and re-layouts: 1.76 us -> 0.01 us
    pallas_call x1, Pallas kernels: 57 us -> 44.6 us  [encode(): pl.pallas_call(functools.partial(enc_kernel, sp), out_shape=(jax.ShapeDty...]
    pallas_call x1, Pallas kernels: 78.2 us -> 81.6 us  [decode(): pl.pallas_call(functools.partial(decode_kernel, sp), out_shape=jax.ShapeD...]
    unnamed x8 -> x2, local copies, waits for them, and re-layouts: 1.76 us -> 0.01 us
where the time goes in v5:
time: 130 us
  Pallas kernels  126 us (97%)
  matrix products  3.69 us (3%)
    pallas_call x1, Pallas kernels, decode(): pl.pallas_call(functools.partial(decode_kernel, sp), out_shape=jax.ShapeD...  81.6 us
    pallas_call x1, Pallas kernels, encode(): pl.pallas_call(functools.partial(enc_kernel, sp), out_shape=(jax.ShapeDty...  44.6 us
    dot_general x1, matrix products, local_program(): return jnp.einsum('cne,ep->cnp', acts, w_out, preferred_element_type=F32)  3.69 us

profile of v5, /device:TPU:0, one launch (start us, length us, event | category | flops | bytes accessed | tf_op | source)
XLA Modules:
  0.0 129.9 jit_solution(5310436245558091051)
XLA Ops:
  0.0 44.6 %encode.1 = (bf16[128,1280]{1,0:T(8,128)(2,1)}, s32[8,2,256]{2,1,0:T(2,128)}, bf16[8,256,512]{2,1,0:T(8,128)(2,1)}) custom-call(s32[2,256]{1,0:T(2,128)} %mask_ref.1, bf16[2,256,1536]{2,1,0:T(8,128)(2,1)} %patches_h.1, bf16[256,1280]{1,0:T(8,128)(2,1)} %enc_pos_h.1, bf16[256,512]{1,0:T(8,128)(2,1)} %dec_pos_h.1, bf16[1536,1280]{1,0:T(8,128)(2,1)} %w_pe_h.1, ...), custom_call_target="tpu_custom_call" | custom-call | tf_op jit(solution)/shard_map/encode/pallas_call | solution.py:318
  44.6 0.0 copy-start
  44.6 81.6 %decode.1 = bf16[2,256,512]{2,1,0:T(8,128)(2,1)} custom-call(bf16[128,1280]{1,0:T(8,128)(2,1)} %get-tuple-element.8.hid_h, bf16[1280,512]{1,0:T(8,128)(2,1)} %w_ed_h.1, s32[8,2,256]{2,1,0:T(2,128)} %get-tuple-element.9.mask_h, bf16[8,256,512]{2,1,0:T(8,128)(2,1)} %get-tuple-element.10.pos_h, bf16[512]{0:T(512)(128)(2,1)} %tok_ref.1, ...), custom_call_target="tpu_custom_call" | custom-call | tf_op jit(solution)/shard_map/decode/pallas_call | solution.py:535
  126.2 0.0 copy-done
  126.2 3.7 %fusion = f32[2,256,1536]{2,1,0:T(8,128)} fusion(bf16[2,256,512]{2,1,0:T(8,128)(2,1)} %decode.1, bf16[512,1536]{1,0:T(8,128)(2,1)S(1)} %copy-done), kind=kOutput, calls=%fused_computation | convolution fusion | flops 805306368 | bytes 5242880 | tf_op jit(solution)/shard_map/cne,ep->cnp/dot_general | solution.py:569
Async XLA Ops:
  44.6 81.6 %copy-start = (bf16[512,1536]{1,0:T(8,128)(2,1)S(1)}, bf16[512,1536]{1,0:T(8,128)(2,1)}, u32[]{:S(2)}) copy-start(bf16[512,1536]{1,0:T(8,128)(2,1)} %param.33) | copy-start | bytes 4718596

commit v6 on v5

--- a/solution.py
+++ b/solution.py
@@ -135,8 +135,7 @@
         x_s[c * cap:(c + 1) * cap, :] = mm(pick2[c * cap:(c + 1) * cap], patches[c]).astype(BF)
     fixed = used * b_pe_ref[...].reshape(1, width).astype(F32) + mm(pick2, enc_pos[...])
     loads[2].wait()
-    for i in range(4):
-        weight(0, i).start()
+    weight(0, 0).start()
     e_src[...] = (mm(x_s[...], w_pe[...]) + fixed).astype(BF)
     late = lax.broadcasted_iota(jnp.int32, (half, cap), 1) - lax.broadcasted_iota(jnp.int32, (half, cap), 0) + half
     for c in range(n_clips):
@@ -182,6 +181,8 @@
                 def _():
                     pltpu.make_async_copy(buf.at[pl.ds(c * step, half)], win.at[pl.ds(last, half)], er).start()
 
+    for i in range(1, 4):
+        weight(0, i).start()
     mask_sends = []
     for k in range(1, sp):
         mask_sends.append(pltpu.make_async_remote_copy(
@@ -411,7 +412,7 @@
             pv_s[c] += mm(pick_of(c, b), pos[b])
         return cc
 
-    lax.fori_loop(0, sp, plain, 0)
+    lax.fori_loop(0, sp, plain, 0, unroll=4)
 
     def far(c, k):
         return pltpu.make_async_remote_copy(
@@ -465,7 +466,7 @@
             vt_s[:, here] = jnp.where(seen, mm(vt_vis, pick), vm_s[:, here].astype(F32)).astype(BF)
             return cc
 
-        lax.fori_loop(0, sp, block, 0)
+        lax.fori_loop(0, sp, block, 0, unroll=8)
         u = put(pick_of(c, me), u_aug, (token + pos[me].astype(F32)).astype(BF))
         u_s[c] = u
         a_own[c] = norm_rows(u)
@@ -502,10 +503,10 @@
             keys_values(1, b, a_all[c, b], k_s, vt_s)
             return cc
 
-        lax.fori_loop(1, n_far, same, 0)
+        lax.fori_loop(1, n_far, same, 0, unroll=True)
         for k in range(n_far):
             near(c, k).wait_recv()
-        lax.fori_loop(0, n_far, other, 0)
+        lax.fori_loop(0, n_far, other, 0, unroll=True)
         attend(1, c)
 
         @pl.when(c == 0)

time: 130 us -> 122 us (0.938)
  Pallas kernels: 126 us -> 118 us
    pallas_call x1, Pallas kernels: 81.6 us -> 73.7 us  [decode(): pl.pallas_call(functools.partial(decode_kernel, sp), out_shape=jax.ShapeD...]
where the time goes in v6:
time: 122 us
  Pallas kernels  118 us (97%)
  matrix products  3.69 us (3%)
    pallas_call x1, Pallas kernels, decode(): pl.pallas_call(functools.partial(decode_kernel, sp), out_shape=jax.ShapeD...  73.7 us
    pallas_call x1, Pallas kernels, encode(): pl.pallas_call(functools.partial(enc_kernel, sp), out_shape=(jax.ShapeDty...  44.6 us
    dot_general x1, matrix products, local_program(): return jnp.einsum('cne,ep->cnp', acts, w_out, preferred_element_type=F32)  3.69 us

profile of v6, /device:TPU:0, one launch (start us, length us, event | category | flops | bytes accessed | tf_op | source)
XLA Modules:
  0.0 122.0 jit_solution(365229285314606571)
XLA Ops:
  0.0 44.6 %encode.1 = (bf16[128,1280]{1,0:T(8,128)(2,1)}, s32[8,2,256]{2,1,0:T(2,128)}, bf16[8,256,512]{2,1,0:T(8,128)(2,1)}) custom-call(s32[2,256]{1,0:T(2,128)} %mask_ref.1, bf16[2,256,1536]{2,1,0:T(8,128)(2,1)} %patches_h.1, bf16[256,1280]{1,0:T(8,128)(2,1)} %enc_pos_h.1, bf16[256,512]{1,0:T(8,128)(2,1)} %dec_pos_h.1, bf16[1536,1280]{1,0:T(8,128)(2,1)} %w_pe_h.1, ...), custom_call_target="tpu_custom_call" | custom-call | tf_op jit(solution)/shard_map/encode/pallas_call | solution.py:319
  44.6 0.0 copy-start
  44.6 73.7 %decode.1 = bf16[2,256,512]{2,1,0:T(8,128)(2,1)} custom-call(bf16[128,1280]{1,0:T(8,128)(2,1)} %get-tuple-element.8.hid_h, bf16[1280,512]{1,0:T(8,128)(2,1)} %w_ed_h.1, s32[8,2,256]{2,1,0:T(2,128)} %get-tuple-element.9.mask_h, bf16[8,256,512]{2,1,0:T(8,128)(2,1)} %get-tuple-element.10.pos_h, bf16[512]{0:T(512)(128)(2,1)} %tok_ref.1, ...), custom_call_target="tpu_custom_call" | custom-call | tf_op jit(solution)/shard_map/decode/pallas_call | solution.py:536
  118.3 0.0 copy-done
  118.3 3.7 %fusion = f32[2,256,1536]{2,1,0:T(8,128)} fusion(bf16[2,256,512]{2,1,0:T(8,128)(2,1)} %decode.1, bf16[512,1536]{1,0:T(8,128)(2,1)S(1)} %copy-done), kind=kOutput, calls=%fused_computation | convolution fusion | flops 805306368 | bytes 5242880 | tf_op jit(solution)/shard_map/cne,ep->cnp/dot_general | solution.py:570
Async XLA Ops:
  44.6 73.7 %copy-start = (bf16[512,1536]{1,0:T(8,128)(2,1)S(1)}, bf16[512,1536]{1,0:T(8,128)(2,1)}, u32[]{:S(2)}) copy-start(bf16[512,1536]{1,0:T(8,128)(2,1)} %param.33) | copy-start | bytes 4718596

commit v7 on v6

--- a/solution.py
+++ b/solution.py
@@ -8,6 +8,7 @@
 from jax.sharding import PartitionSpec as P
 
 KEEP_DIV = 8
+HEADS_PER_STEP = 8
 
 
 BF = jnp.bfloat16
@@ -48,41 +49,35 @@
         row_head = lax.broadcasted_iota(jnp.int32, (256, rows), 0) // hd
         return jnp.where(row_head == h - g * group, qg, jnp.zeros_like(qg)), pl.multiple_of(g * 256, 256)
 
-    def scores(h, slot):
-        qz, g0 = q_of(h)
-        top = None
+    def turn(nxt, nxt_slot, h, slot, top):
+        qz, g0 = q_of(nxt)
+        next_top = total = acc = None
+        if h is not None:
+            m = jnp.max(top, axis=0, keepdims=True) * c2
+            v0 = pl.multiple_of(h * hd, hd)
         for j in range(n_chunks):
-            s = mm(k_s[j * chunk:(j + 1) * chunk, pl.ds(g0, 256)], qz)
-            s_s[slot, j * chunk:(j + 1) * chunk, :] = s
+            at = slice(j * chunk, (j + 1) * chunk)
+            s = mm(k_s[at, pl.ds(g0, 256)], qz)
+            s_s[nxt_slot, at, :] = s
             t = jnp.max(s.reshape(chunk // 8, 8, rows), axis=0)
-            top = t if top is None else jnp.maximum(top, t)
+            next_top = t if next_top is None else jnp.maximum(next_top, t)
+            if h is not None:
+                e = jnp.exp2(s_s[slot, at, :] * c2 - m)
+                t = jnp.sum(e.reshape(chunk // 8, 8, rows), axis=0)
+                total = t if total is None else total + t
+                a = mm(vt_s[pl.ds(v0, hd), at], e.astype(BF))
+                acc = a if acc is None else acc + a
+        if h is not None:
+            o_s[pl.ds(v0, hd), :] = (acc / jnp.sum(total, axis=0, keepdims=True)).astype(BF)
+        return next_top
+
+    def body(i, top):
+        for u in range(HEADS_PER_STEP):
+            h = HEADS_PER_STEP * i + u
+            top = turn(jnp.minimum(h + 1, heads - 1), (u + 1) % 2, h, u % 2, top)
         return top
 
-    def finish(h, slot, top):
-        m = jnp.max(top, axis=0, keepdims=True) * c2
-        total = None
-        acc = None
-        v0 = pl.multiple_of(h * hd, hd)
-        for j in range(n_chunks):
-            e = jnp.exp2(s_s[slot, j * chunk:(j + 1) * chunk, :] * c2 - m)
-            t = jnp.sum(e.reshape(chunk // 8, 8, rows), axis=0)
-            total = t if total is None else total + t
-            a = mm(vt_s[pl.ds(v0, hd), j * chunk:(j + 1) * chunk], e.astype(BF))
-            acc = a if acc is None else acc + a
-        denom = jnp.sum(total, axis=0, keepdims=True)
-        o_s[pl.ds(v0, hd), :] = (acc / denom).astype(BF)
-
-    first = scores(0, 0)
-
-    def body(i, top0):
-        h = 2 * i
-        top1 = scores(h + 1, 1)
-        finish(h, 0, top0)
-        nxt = scores(jnp.minimum(h + 2, heads - 1), 0)
-        finish(h + 1, 1, top1)
-        return nxt
-
-    lax.fori_loop(0, heads // 2, body, first)
+    lax.fori_loop(0, heads // HEADS_PER_STEP, body, turn(0, 0, None, None, None))
 
 
 def enc_kernel(sp, mask_ref, patches_h, enc_pos_h, dec_pos_h, w_pe_h, b_pe_ref, qkv_h, proj_h, up_h, down_h,

time: 122 us -> 118 us (0.967)
  Pallas kernels: 118 us -> 114 us
    pallas_call x1, Pallas kernels: 73.7 us -> 69.7 us  [decode(): pl.pallas_call(functools.partial(decode_kernel, sp), out_shape=jax.ShapeD...]
where the time goes in v7:
time: 118 us
  Pallas kernels  114 us (97%)
  matrix products  3.69 us (3%)
    pallas_call x1, Pallas kernels, decode(): pl.pallas_call(functools.partial(decode_kernel, sp), out_shape=jax.ShapeD...  69.7 us
    pallas_call x1, Pallas kernels, encode(): pl.pallas_call(functools.partial(enc_kernel, sp), out_shape=(jax.ShapeDty...  44.6 us
    dot_general x1, matrix products, local_program(): return jnp.einsum('cne,ep->cnp', acts, w_out, preferred_element_type=F32)  3.69 us

profile of v7, /device:TPU:0, one launch (start us, length us, event | category | flops | bytes accessed | tf_op | source)
XLA Modules:
  0.0 118.0 jit_solution(6513106791302088342)
XLA Ops:
  0.0 44.6 %encode.1 = (bf16[128,1280]{1,0:T(8,128)(2,1)}, s32[8,2,256]{2,1,0:T(2,128)}, bf16[8,256,512]{2,1,0:T(8,128)(2,1)}) custom-call(s32[2,256]{1,0:T(2,128)} %mask_ref.1, bf16[2,256,1536]{2,1,0:T(8,128)(2,1)} %patches_h.1, bf16[256,1280]{1,0:T(8,128)(2,1)} %enc_pos_h.1, bf16[256,512]{1,0:T(8,128)(2,1)} %dec_pos_h.1, bf16[1536,1280]{1,0:T(8,128)(2,1)} %w_pe_h.1, ...), custom_call_target="tpu_custom_call" | custom-call | tf_op jit(solution)/shard_map/encode/pallas_call | solution.py:314
  44.6 0.0 copy-start
  44.6 69.7 %decode.1 = bf16[2,256,512]{2,1,0:T(8,128)(2,1)} custom-call(bf16[128,1280]{1,0:T(8,128)(2,1)} %get-tuple-element.8.hid_h, bf16[1280,512]{1,0:T(8,128)(2,1)} %w_ed_h.1, s32[8,2,256]{2,1,0:T(2,128)} %get-tuple-element.9.mask_h, bf16[8,256,512]{2,1,0:T(8,128)(2,1)} %get-tuple-element.10.pos_h, bf16[512]{0:T(512)(128)(2,1)} %tok_ref.1, ...), custom_call_target="tpu_custom_call" | custom-call | tf_op jit(solution)/shard_map/decode/pallas_call | solution.py:531
  114.3 0.0 copy-done
  114.4 3.7 %fusion = f32[2,256,1536]{2,1,0:T(8,128)} fusion(bf16[2,256,512]{2,1,0:T(8,128)(2,1)} %decode.1, bf16[512,1536]{1,0:T(8,128)(2,1)S(1)} %copy-done), kind=kOutput, calls=%fused_computation | convolution fusion | flops 805306368 | bytes 5242880 | tf_op jit(solution)/shard_map/cne,ep->cnp/dot_general | solution.py:565
Async XLA Ops:
  44.6 69.8 %copy-start = (bf16[512,1536]{1,0:T(8,128)(2,1)S(1)}, bf16[512,1536]{1,0:T(8,128)(2,1)}, u32[]{:S(2)}) copy-start(bf16[512,1536]{1,0:T(8,128)(2,1)} %param.33) | copy-start | bytes 4718596

commit v8 on v7

--- a/solution.py
+++ b/solution.py
@@ -255,7 +255,7 @@
             p_s[i] = (e / jnp.sum(e, axis=-1, keepdims=True)).astype(BF)
             return cc
 
-        lax.fori_loop(0, heads, soft, 0, unroll=4)
+        lax.fori_loop(0, heads, soft, 0, unroll=16)
         for h in range(heads):
             o_s[h * hd:(h + 1) * hd, :] = mm(qkv_s[2 * width + h * hd:2 * width + (h + 1) * hd, :], p_s[h], NT).astype(BF)
         weight(l, 1).wait()

time: 118 us -> 116 us (0.983)
    pallas_call x1, Pallas kernels: 44.6 us -> 42.7 us  [encode(): pl.pallas_call(functools.partial(enc_kernel, sp), out_shape=(jax.ShapeDty...]
where the time goes in v8:
time: 116 us
  Pallas kernels  113 us (97%)
  matrix products  3.69 us (3%)
    pallas_call x1, Pallas kernels, decode(): pl.pallas_call(functools.partial(decode_kernel, sp), out_shape=jax.ShapeD...  69.8 us
    pallas_call x1, Pallas kernels, encode(): pl.pallas_call(functools.partial(enc_kernel, sp), out_shape=(jax.ShapeDty...  42.7 us
    dot_general x1, matrix products, local_program(): return jnp.einsum('cne,ep->cnp', acts, w_out, preferred_element_type=F32)  3.69 us

profile of v8, /device:TPU:0, one launch (start us, length us, event | category | flops | bytes accessed | tf_op | source)
XLA Modules:
  0.0 116.2 jit_solution(18352850634993067548)
XLA Ops:
  0.0 42.7 %encode.1 = (bf16[128,1280]{1,0:T(8,128)(2,1)}, s32[8,2,256]{2,1,0:T(2,128)}, bf16[8,256,512]{2,1,0:T(8,128)(2,1)}) custom-call(s32[2,256]{1,0:T(2,128)} %mask_ref.1, bf16[2,256,1536]{2,1,0:T(8,128)(2,1)} %patches_h.1, bf16[256,1280]{1,0:T(8,128)(2,1)} %enc_pos_h.1, bf16[256,512]{1,0:T(8,128)(2,1)} %dec_pos_h.1, bf16[1536,1280]{1,0:T(8,128)(2,1)} %w_pe_h.1, ...), custom_call_target="tpu_custom_call" | custom-call | tf_op jit(solution)/shard_map/encode/pallas_call | solution.py:314
  42.7 0.0 copy-start
  42.8 69.8 %decode.1 = bf16[2,256,512]{2,1,0:T(8,128)(2,1)} custom-call(bf16[128,1280]{1,0:T(8,128)(2,1)} %get-tuple-element.8.hid_h, bf16[1280,512]{1,0:T(8,128)(2,1)} %w_ed_h.1, s32[8,2,256]{2,1,0:T(2,128)} %get-tuple-element.9.mask_h, bf16[8,256,512]{2,1,0:T(8,128)(2,1)} %get-tuple-element.10.pos_h, bf16[512]{0:T(512)(128)(2,1)} %tok_ref.1, ...), custom_call_target="tpu_custom_call" | custom-call | tf_op jit(solution)/shard_map/decode/pallas_call | solution.py:531
  112.5 0.0 copy-done
  112.5 3.7 %fusion = f32[2,256,1536]{2,1,0:T(8,128)} fusion(bf16[2,256,512]{2,1,0:T(8,128)(2,1)} %decode.1, bf16[512,1536]{1,0:T(8,128)(2,1)S(1)} %copy-done), kind=kOutput, calls=%fused_computation | convolution fusion | flops 805306368 | bytes 5242880 | tf_op jit(solution)/shard_map/cne,ep->cnp/dot_general | solution.py:565
Async XLA Ops:
  42.7 69.8 %copy-start = (bf16[512,1536]{1,0:T(8,128)(2,1)S(1)}, bf16[512,1536]{1,0:T(8,128)(2,1)}, u32[]{:S(2)}) copy-start(bf16[512,1536]{1,0:T(8,128)(2,1)} %param.33) | copy-start | bytes 4718596

commit v9 on v8

--- a/solution.py
+++ b/solution.py
@@ -59,13 +59,17 @@
             at = slice(j * chunk, (j + 1) * chunk)
             s = mm(k_s[at, pl.ds(g0, 256)], qz)
             s_s[nxt_slot, at, :] = s
-            t = jnp.max(s.reshape(chunk // 8, 8, rows), axis=0)
-            next_top = t if next_top is None else jnp.maximum(next_top, t)
+            for r in range(0, chunk, 64):
+                t = jnp.max(s[r:r + 64].reshape(8, 8, rows), axis=0)
+                next_top = t if next_top is None else jnp.maximum(next_top, t)
             if h is not None:
-                e = jnp.exp2(s_s[slot, at, :] * c2 - m)
-                t = jnp.sum(e.reshape(chunk // 8, 8, rows), axis=0)
-                total = t if total is None else total + t
-                a = mm(vt_s[pl.ds(v0, hd), at], e.astype(BF))
+                weights = []
+                for r in range(j * chunk, (j + 1) * chunk, 64):
+                    e = jnp.exp2(s_s[slot, r:r + 64, :] * c2 - m)
+                    t = jnp.sum(e.reshape(8, 8, rows), axis=0)
+                    total = t if total is None else total + t
+                    weights.append(e.astype(BF))
+                a = mm(vt_s[pl.ds(v0, hd), at], jnp.concatenate(weights, axis=0))
                 acc = a if acc is None else acc + a
         if h is not None:
             o_s[pl.ds(v0, hd), :] = (acc / jnp.sum(total, axis=0, keepdims=True)).astype(BF)
@@ -407,7 +411,7 @@
             pv_s[c] += mm(pick_of(c, b), pos[b])
         return cc
 
-    lax.fori_loop(0, sp, plain, 0, unroll=4)
+    lax.fori_loop(0, sp, plain, 0, unroll=8)
 
     def far(c, k):
         return pltpu.make_async_remote_copy(

time: 116 us -> 116 us (level)
  no operation moved by 1% of the time
where the time goes in v9:
time: 116 us
  Pallas kernels  112 us (97%)
  matrix products  3.69 us (3%)
    pallas_call x1, Pallas kernels, decode(): pl.pallas_call(functools.partial(decode_kernel, sp), out_shape=jax.ShapeD...  69.1 us
    pallas_call x1, Pallas kernels, encode(): pl.pallas_call(functools.partial(enc_kernel, sp), out_shape=(jax.ShapeDty...  42.9 us
    dot_general x1, matrix products, local_program(): return jnp.einsum('cne,ep->cnp', acts, w_out, preferred_element_type=F32)  3.69 us

profile of v9, /device:TPU:0, one launch (start us, length us, event | category | flops | bytes accessed | tf_op | source)
XLA Modules:
  0.0 115.8 jit_solution(15598018017387036626)
XLA Ops:
  0.0 42.9 %encode.1 = (bf16[128,1280]{1,0:T(8,128)(2,1)}, s32[8,2,256]{2,1,0:T(2,128)}, bf16[8,256,512]{2,1,0:T(8,128)(2,1)}) custom-call(s32[2,256]{1,0:T(2,128)} %mask_ref.1, bf16[2,256,1536]{2,1,0:T(8,128)(2,1)} %patches_h.1, bf16[256,1280]{1,0:T(8,128)(2,1)} %enc_pos_h.1, bf16[256,512]{1,0:T(8,128)(2,1)} %dec_pos_h.1, bf16[1536,1280]{1,0:T(8,128)(2,1)} %w_pe_h.1, ...), custom_call_target="tpu_custom_call" | custom-call | tf_op jit(solution)/shard_map/encode/pallas_call | solution.py:318
  42.9 0.0 copy-start
  42.9 69.1 %decode.1 = bf16[2,256,512]{2,1,0:T(8,128)(2,1)} custom-call(bf16[128,1280]{1,0:T(8,128)(2,1)} %get-tuple-element.8.hid_h, bf16[1280,512]{1,0:T(8,128)(2,1)} %w_ed_h.1, s32[8,2,256]{2,1,0:T(2,128)} %get-tuple-element.9.mask_h, bf16[8,256,512]{2,1,0:T(8,128)(2,1)} %get-tuple-element.10.pos_h, bf16[512]{0:T(512)(128)(2,1)} %tok_ref.1, ...), custom_call_target="tpu_custom_call" | custom-call | tf_op jit(solution)/shard_map/decode/pallas_call | solution.py:535
  112.1 0.0 copy-done
  112.1 3.7 %fusion = f32[2,256,1536]{2,1,0:T(8,128)} fusion(bf16[2,256,512]{2,1,0:T(8,128)(2,1)} %decode.1, bf16[512,1536]{1,0:T(8,128)(2,1)S(1)} %copy-done), kind=kOutput, calls=%fused_computation | convolution fusion | flops 805306368 | bytes 5242880 | tf_op jit(solution)/shard_map/cne,ep->cnp/dot_general | solution.py:569
Async XLA Ops:
  42.9 69.2 %copy-start = (bf16[512,1536]{1,0:T(8,128)(2,1)S(1)}, bf16[512,1536]{1,0:T(8,128)(2,1)}, u32[]{:S(2)}) copy-start(bf16[512,1536]{1,0:T(8,128)(2,1)} %param.33) | copy-start | bytes 4718596
